TPU v7x, 128 devices: a whole 4x4x4 slice. The times are simulated.
128 devices in a mesh: dp: 1, tx: 16 (over z, y), tyz: 8 (over x, core).
Axes of the slice: x: 4, y: 4, z: 4, core: 2. Of those that a mesh axis runs over, the one named last changes fastest.
Arguments:
- residual: bfloat16 [8192, 5120], P('dp', ('tx', 'tyz'))
- ln_scale: bfloat16 [5120], P(('tx', 'tyz'))
- w_query: bfloat16 [5120, 5120], P('tx', 'tyz')
- w_key: bfloat16 [5120, 128], P('tx')
- w_value: bfloat16 [5120, 128], P('tx')
- w_gate: bfloat16 [5120, 20480], P('tx', 'tyz')
- w_up: bfloat16 [5120, 20480], P('tx', 'tyz')
- w_out: bfloat16 [5120, 5120], P('tyz', 'tx')
- w_down: bfloat16 [20480, 5120], P('tyz', 'tx')
- k_cache: bfloat16 [8192, 64, 128], P(('dp', 'tx', 'tyz'))
- v_cache: bfloat16 [8192, 64, 128], P(('dp', 'tx', 'tyz'))
- lengths: int32 [8192], P(('dp', 'tx', 'tyz'))
Outputs:
- output 1: bfloat16 [8192, 5120], P('dp', ('tx', 'tyz'))
- output 2: bfloat16 [8192, 64, 128], P(('dp', 'tx', 'tyz'))
- output 3: bfloat16 [8192, 64, 128], P(('dp', 'tx', 'tyz'))
All inputs are finite; a program needn't handle non-finite values.
Results may differ from a plain program's by a relative error of at most 0.02.
Values are sent between devices in bfloat16 or wider.
A program may use at most 1 GiB of HBM per device.

v0:
```python
import jax
import jax.numpy as jnp
from jax import lax
from jax.sharding import PartitionSpec as P

LN_EPS = 1e-5
ROPE_BASE = 10000.0


def rope_rotate(vectors, positions):
    head_dim = vectors.shape[-1]
    half_dim = head_dim // 2
    inv_freq = ROPE_BASE ** (-2.0 * jnp.arange(half_dim, dtype=jnp.float32) / head_dim)
    angles = positions.astype(jnp.float32)[:, None] * inv_freq[None, :]
    bcast_shape = (angles.shape[0],) + (1,) * (vectors.ndim - 2) + (half_dim,)
    cos_part = jnp.cos(angles).reshape(bcast_shape)
    sin_part = jnp.sin(angles).reshape(bcast_shape)
    vec_f32 = vectors.astype(jnp.float32)
    first_half = vec_f32[..., :half_dim]
    second_half = vec_f32[..., half_dim:]
    rotated = jnp.concatenate([first_half * cos_part - second_half * sin_part, second_half * cos_part + first_half * sin_part], axis=-1)
    return rotated.astype(jnp.bfloat16)


def attend_rows(query_rot, key_rot, value_new, k_cache, v_cache, lengths):
    positions = jnp.arange(k_cache.shape[1], dtype=jnp.int32)
    write_mask = (positions[None, :] == lengths[:, None])[:, :, None]
    k_updated = jnp.where(write_mask, key_rot[:, None, :], k_cache)
    v_updated = jnp.where(write_mask, value_new[:, None, :], v_cache)
    scores = jnp.einsum('rhd,rtd->rht', query_rot, k_updated, preferred_element_type=jnp.float32) * (query_rot.shape[-1] ** -0.5)
    valid_mask = (positions[None, :] <= lengths[:, None])[:, None, :]
    scores = jnp.where(valid_mask, scores, -1e30)
    attn_probs = jax.nn.softmax(scores, axis=-1).astype(jnp.bfloat16)
    attended = jnp.einsum('rht,rtd->rhd', attn_probs, v_updated, preferred_element_type=jnp.float32).astype(jnp.bfloat16)
    return attended, k_updated, v_updated


def solution(mesh):
    tx_size = mesh.shape['tx']
    tyz_size = mesh.shape['tyz']
    row_axes = ('dp', 'tx', 'tyz')

    def decode_layer(residual, ln_scale, w_query, w_key, w_value, w_gate, w_up, w_out, w_down, k_cache, v_cache, lengths):
        model_dim = residual.shape[1] * tx_size * tyz_size
        rows_local = k_cache.shape[0]
        head_dim = w_key.shape[1]
        res_f32 = residual.astype(jnp.float32)
        row_stats = jnp.stack([jnp.sum(res_f32, axis=1), jnp.sum(jnp.square(res_f32), axis=1)])
        row_stats = lax.psum(row_stats, ('tx', 'tyz'))
        row_mean = row_stats[0] / model_dim
        row_var = row_stats[1] / model_dim - jnp.square(row_mean)
        normed = ((res_f32 - row_mean[:, None]) * lax.rsqrt(row_var + LN_EPS)[:, None] * ln_scale.astype(jnp.float32)).astype(jnp.bfloat16)
        normed_tx = lax.all_gather(normed, 'tyz', axis=1, tiled=True)
        gate_part = jnp.dot(normed_tx, w_gate, preferred_element_type=jnp.float32).astype(jnp.bfloat16)
        up_part = jnp.dot(normed_tx, w_up, preferred_element_type=jnp.float32).astype(jnp.bfloat16)
        query_part = jnp.dot(normed_tx, w_query, preferred_element_type=jnp.float32).astype(jnp.bfloat16)
        key_part = jnp.dot(normed_tx, w_key, preferred_element_type=jnp.float32).astype(jnp.bfloat16)
        value_part = jnp.dot(normed_tx, w_value, preferred_element_type=jnp.float32).astype(jnp.bfloat16)
        gate_sum = lax.psum_scatter(gate_part, 'tx', scatter_dimension=1, tiled=True)
        up_sum = lax.psum_scatter(up_part, 'tx', scatter_dimension=1, tiled=True)
        mlp_act = (jax.nn.silu(gate_sum.astype(jnp.float32)) * up_sum.astype(jnp.float32)).astype(jnp.bfloat16)
        act_full = lax.all_gather(mlp_act, 'tx', axis=1, tiled=True)
        query_rows = lax.psum_scatter(query_part, 'tx', scatter_dimension=0, tiled=True)
        key_rows = lax.psum_scatter(key_part, 'tx', scatter_dimension=0, tiled=True)
        value_rows = lax.psum_scatter(value_part, 'tx', scatter_dimension=0, tiled=True)
        query_mine = lax.all_to_all(query_rows.reshape(query_rows.shape[0], -1, head_dim), 'tyz', 0, 1, tiled=True)
        row_start = lax.axis_index('tyz') * rows_local
        key_mine = lax.dynamic_slice_in_dim(key_rows, row_start, rows_local, axis=0)
        value_mine = lax.dynamic_slice_in_dim(value_rows, row_start, rows_local, axis=0)
        query_rot = rope_rotate(query_mine, lengths)
        key_rot = rope_rotate(key_mine, lengths)
        attended, k_updated, v_updated = attend_rows(query_rot, key_rot, value_mine, k_cache, v_cache, lengths)
        attended_heads = lax.all_to_all(attended, 'tyz', 1, 0, tiled=True)
        attended_all = lax.all_gather(attended_heads, 'tx', axis=0, tiled=True)
        attended_flat = attended_all.reshape(attended_all.shape[0], -1)
        block_part = jnp.dot(attended_flat, w_out, preferred_element_type=jnp.float32) + jnp.dot(act_full, w_down, preferred_element_type=jnp.float32)
        block_sum = lax.psum_scatter(block_part.astype(jnp.bfloat16), 'tyz', scatter_dimension=1, tiled=True)
        new_resid = (res_f32 + block_sum.astype(jnp.float32)).astype(jnp.bfloat16)
        return new_resid, k_updated, v_updated

    in_specs = (P('dp', ('tx', 'tyz')), P(('tx', 'tyz')), P('tx', 'tyz'), P('tx', None), P('tx', None), P('tx', 'tyz'), P('tx', 'tyz'), P('tyz', 'tx'), P('tyz', 'tx'), P(row_axes, None, None), P(row_axes, None, None), P(row_axes))
    out_specs = (P('dp', ('tx', 'tyz')), P(row_axes, None, None), P(row_axes, None, None))
    return jax.shard_map(decode_layer, mesh=mesh, in_specs=in_specs, out_specs=out_specs, check_vma=False)
```

profile of v0, /device:TPU:1, one launch (start us, length us, event | category | flops | bytes accessed | tf_op | source)
XLA Modules:
  0.0 1327.6 jit_solution(15494480899031723739)
XLA Ops:
  10.2 152.1 %all-reduce.2.cloned.1.call-done = f32[2,8192]{1,0:T(2,128)} async-done(((f32[2,8192]{1,0:T(2,128)}), f32[2,8192]{1,0:T(2,128)}) %all-reduce.2.cloned.1.call-update) | async-done | bytes 65552 | tf_op jit(solution)/shard_map/psum | solution.py:49
  163.3 2.2 fusion.13
  165.5 35.2 %all-gather.4.cloned.1.call-done = bf16[8192,320]{0,1:T(8,128)(2,1)} async-done(((bf16[8192,40]{0,1:T(8,128)(2,1)}), bf16[8192,320]{0,1:T(8,128)(2,1)}) %all-gather.4.cloned.1.call-update) | async-done | bytes 5242896 | tf_op jit(solution)/shard_map/all_gather | solution.py:53
  200.7 5.7 convolution_convert_fusion.3
  207.3 5.7 convolution_convert_fusion.4
  214.0 10.5 convolution_convert_fusion.2
  224.8 29.0 %convolution_convert_fusion = bf16[8192,2560]{0,1:T(8,128)(2,1)} fusion(bf16[8192,320]{0,1:T(8,128)(2,1)} %all-gather.4.cloned.1.call-done, bf16[320,2560]{1,0:T(8,128)(2,1)S(1)} %copy-done), kind=kOutput, calls=%fused_computation.1 | convolution fusion | flops 13442744320 | bytes 48824320 | tf_op jit(solution)/shard_map/dot_general | solution.py:55
  255.2 29.1 %convolution_convert_fusion.1 = bf16[8192,2560]{0,1:T(8,128)(2,1)} fusion(bf16[8192,320]{0,1:T(8,128)(2,1)} %all-gather.4.cloned.1.call-done, bf16[320,2560]{1,0:T(8,128)(2,1)S(1)} %copy-done.8), kind=kOutput, calls=%fused_computation.2 | convolution fusion | flops 13442744320 | bytes 48824320 | tf_op jit(solution)/shard_map/dot_general | solution.py:54
  285.2 72.4 %reduce-scatter.9.cloned.1.call-done = bf16[512,128]{1,0:T(8,128)(2,1)} async-done(((bf16[8192,128]{1,0:T(8,128)(2,1)}), bf16[512,128]{1,0:T(8,128)(2,1)}) %reduce-scatter.9.cloned.1.call-update) | async-done | bytes 131088 | tf_op jit(solution)/shard_map/reduce_scatter | solution.py:64
  358.3 92.5 %reduce-scatter.7.cloned.1.call-done = bf16[512,640]{1,0:T(8,128)(2,1)} async-done(((bf16[8192,640]{1,0:T(8,128)(2,1)}), bf16[512,640]{1,0:T(8,128)(2,1)}) %reduce-scatter.7.cloned.1.call-update) | async-done | bytes 655376 | tf_op jit(solution)/shard_map/reduce_scatter | solution.py:63
  453.6 6.1 all-to-all-start
  459.9 3.6 broadcast_select_fusion.1
  463.5 10.8 all-to-all-done
  479.9 6.7 convolution_convert_fusion.5
  486.8 14.4 %all_to_all.27 = bf16[64,40,128]{2,0,1:T(8,128)(2,1)S(1)} all-to-all(bf16[64,40,128]{2,0,1:T(8,128)(2,1)S(1)} %copy.37), channel_id=1, replica_groups=mesh['dp'=1,'tx'=16,'tyz'=8] {'tyz'}, dimensions={1} | all-to-all | bytes 1310720 | tf_op jit(solution)/shard_map/all_to_all | solution.py:73
  502.2 189.4 %reduce-scatter.15.cloned.1.call-done = bf16[8192,160]{0,1:T(8,128)(2,1)} async-done(((bf16[8192,2560]{0,1:T(8,128)(2,1)}), bf16[8192,160]{0,1:T(8,128)(2,1)}) %reduce-scatter.15.cloned.1.call-update) | async-done | bytes 2621456 | tf_op jit(solution)/shard_map/reduce_scatter | solution.py:60
  691.6 240.4 %reduce-scatter.13.cloned.1.call-done = bf16[8192,160]{0,1:T(8,128)(2,1)} async-done(((bf16[8192,2560]{0,1:T(8,128)(2,1)}), bf16[8192,160]{0,1:T(8,128)(2,1)}) %reduce-scatter.13.cloned.1.call-update) | async-done | bytes 2621456 | tf_op jit(solution)/shard_map/reduce_scatter | solution.py:59
  932.0 5.6 fusion.6
  938.0 76.8 %all-gather.6.cloned.1.call-done = bf16[8192,5,128]{2,0,1:T(8,128)(2,1)} async-done(((bf16[512,5,128]{2,0,1:T(8,128)(2,1)}), bf16[8192,5,128]{2,0,1:T(8,128)(2,1)}) %all-gather.6.cloned.1.call-update) | async-done | bytes 10485776 | tf_op jit(solution)/shard_map/all_gather | solution.py:74
  1014.8 14.2 %copy.39 = bf16[8192,5,128]{0,2,1:T(8,128)(2,1)} copy(bf16[8192,5,128]{2,0,1:T(8,128)(2,1)} %all-gather.6.cloned.1.call-done) | data formatting | bytes 20971520 | tf_op jit(solution)/shard_map/all_gather | solution.py:74
  1029.0 10.9 fusion.31
  1039.9 216.6 %all-gather.8.cloned.1.call-done = bf16[8192,2560]{0,1:T(8,128)(2,1)} async-done(((bf16[8192,160]{0,1:T(8,128)(2,1)}), bf16[8192,2560]{0,1:T(8,128)(2,1)}) %all-gather.8.cloned.1.call-update) | async-done | bytes 41943056 | tf_op jit(solution)/shard_map/all_gather | solution.py:62
  1256.5 24.7 %fusion.1 = bf16[8192,320]{0,1:T(8,128)(2,1)} fusion(f32[8192,320]{0,1:T(8,128)} %fusion.31, bf16[2560,320]{0,1:T(8,128)(2,1)S(1)} %copy-done.9, bf16[8192,2560]{0,1:T(8,128)(2,1)} %all-gather.8.cloned.1.call-done), kind=kOutput, calls=%fused_computation.5 | convolution fusion | flops 13427015680 | bytes 59310080 | tf_op jit(solution)/shard_map/dot_general | solution.py:76
  1281.3 37.4 %reduce-scatter.17.cloned.1.call-done = bf16[8192,40]{0,1:T(8,128)(2,1)} async-done(((bf16[8192,320]{0,1:T(8,128)(2,1)}), bf16[8192,40]{0,1:T(8,128)(2,1)}) %reduce-scatter.17.cloned.1.call-update) | async-done | bytes 655376 | tf_op jit(solution)/shard_map/reduce_scatter | solution.py:77
  (66 shorter events, 21.1 us)
Async XLA Ops:
  7.2 217.6 %copy-start = (bf16[320,2560]{1,0:T(8,128)(2,1)S(1)}, bf16[320,2560]{1,0:T(8,128)(2,1)}, u32[]{:S(2)}) copy-start(bf16[320,2560]{1,0:T(8,128)(2,1)} %param.18) | copy-start | bytes 4915204
  7.2 193.5 %copy-start.5 = (bf16[320,128]{1,0:T(8,128)(2,1)S(1)}, bf16[320,128]{1,0:T(8,128)(2,1)}, u32[]{:S(2)}) copy-start(bf16[320,128]{1,0:T(8,128)(2,1)} %param.16) | copy-start | bytes 245764
  7.2 155.1 %all-reduce.2.cloned.1.call-start = ((), (), s32[]{:S(2)}) async-start(), calls=%async_computation.8 | async-start | bytes 131072 | tf_op jit(solution)/shard_map/psum | solution.py:49
  9.4 191.3 %all-gather.4.cloned.1.call-start = ((), (), s32[]{:S(2)}) async-start(), calls=%async_computation.9 | async-start | bytes 5898240 | tf_op jit(solution)/shard_map/all_gather | solution.py:53
  165.5 119.7 %reduce-scatter.11.cloned.1.call-start = ((), (), s32[]{:S(2)}) async-start(), calls=%async_computation.12 | async-start | bytes 2228224 | tf_op jit(solution)/shard_map/reduce_scatter | solution.py:65
  206.4 0.9 copy-start.6
  206.4 151.1 %reduce-scatter.9.cloned.1.call-start = ((), (), s32[]{:S(2)}) async-start(), calls=%async_computation.11 | async-start | bytes 2228224 | tf_op jit(solution)/shard_map/reduce_scatter | solution.py:64
  213.0 1.0 copy-start.10
  213.0 237.8 %reduce-scatter.7.cloned.1.call-start = ((), (), s32[]{:S(2)}) async-start(), calls=%async_computation.10 | async-start | bytes 11141120 | tf_op jit(solution)/shard_map/reduce_scatter | solution.py:63
  224.5 467.1 %reduce-scatter.15.cloned.1.call-start = ((), (), s32[]{:S(2)}) async-start(), calls=%async_computation.15 | async-start | bytes 44564480 | tf_op jit(solution)/shard_map/reduce_scatter | solution.py:60
  253.8 1.4 copy-start.8
  253.8 678.1 %reduce-scatter.13.cloned.1.call-start = ((), (), s32[]{:S(2)}) async-start(), calls=%async_computation.14 | async-start | bytes 44564480 | tf_op jit(solution)/shard_map/reduce_scatter | solution.py:59
  284.4 0.7 copy-start.7
  453.6 20.8 %all-to-all-start = ((bf16[512,5,128]{2,1,0:T(8,128)(2,1)}), bf16[512,5,128]{2,1,0:T(8,128)(2,1)S(1)}, u32[]{:S(2)}, u32[]{:S(2)}) async-start(bf16[512,5,128]{2,1,0:T(8,128)(2,1)} %copy.32), calls=%async_computation.1 | async-start | bytes 2097152 | tf_op jit(solution)/shard_map/all_to_all | solution.py:66
  459.6 555.2 %all-gather.6.cloned.1.call-start = ((), (), s32[]{:S(2)}) async-start(), calls=%async_computation.13 | async-start | bytes 11141120 | tf_op jit(solution)/shard_map/all_gather | solution.py:74
  463.5 14.5 %copy-start.3 = (bf16[64,64,128]{2,1,0:T(8,128)(2,1)}, bf16[64,64,128]{2,1,0:T(8,128)(2,1)S(1)}, u32[]{:S(2)}) copy-start(bf16[64,64,128]{2,1,0:T(8,128)(2,1)S(1)} %get-tuple-element.13) | copy-start | bytes 3145732
  502.1 754.4 %all-gather.8.cloned.1.call-start = ((), (), s32[]{:S(2)}) async-start(), calls=%async_computation.16 | async-start | bytes 44564480 | tf_op jit(solution)/shard_map/all_gather | solution.py:62
  937.6 91.4 %copy-start.4 = (bf16[640,320]{0,1:T(8,128)(2,1)S(1)}, bf16[640,320]{0,1:T(8,128)(2,1)}, u32[]{:S(2)}) copy-start(bf16[640,320]{0,1:T(8,128)(2,1)} %param.19) | copy-start | bytes 1228804
  937.7 381.0 %reduce-scatter.17.cloned.1.call-start = ((), (), s32[]{:S(2)}) async-start(), calls=%async_computation.17 | async-start | bytes 5898240 | tf_op jit(solution)/shard_map/reduce_scatter | solution.py:77
  1029.0 227.5 %copy-start.9 = (bf16[2560,320]{0,1:T(8,128)(2,1)S(1)}, bf16[2560,320]{0,1:T(8,128)(2,1)}, u32[]{:S(2)}) copy-start(bf16[2560,320]{0,1:T(8,128)(2,1)} %param.20) | copy-start | bytes 4915204
  1281.2 37.4 %copy-start.2 = (bf16[8192,40]{0,1:T(8,128)(2,1)S(1)}, bf16[8192,40]{0,1:T(8,128)(2,1)}, u32[]{:S(2)}) copy-start(bf16[8192,40]{0,1:T(8,128)(2,1)} %param.12) | copy-start | bytes 1966084
  1281.3 39.5 %copy-start.1 = (bf16[320,2560]{1,0:T(8,128)(2,1)S(1)}, bf16[320,2560]{1,0:T(8,128)(2,1)}, u32[]{:S(2)}) copy-start(bf16[320,2560]{1,0:T(8,128)(2,1)} %param.18) | copy-start | bytes 4915204
Sparse Core Ops, SparseCore 0:
  13.3 148.8 all-reduce.1
  165.6 35.0 all-gather.3
  206.5 73.3 reduce-scatter.10
  283.0 74.4 reduce-scatter.8
  360.8 89.9 reduce-scatter.6
  454.2 237.3 reduce-scatter.14
  695.1 236.8 reduce-scatter.12
  934.7 80.0 all-gather.5
  1016.9 239.5 all-gather.7
  1281.4 37.2 reduce-scatter.16
where the time goes:
time: 1330 us
  waiting for transfers between devices  1120 us (84%)
  matrix products  125 us (9%)
  local copies, waits for them, and re-layouts  22.5 us (2%)
  other arithmetic  20.3 us (2%)
  blocking collectives  14.4 us (1%)
  between operations  14.3 us (1%)
    reduce_scatter x1, waiting for transfers between devices, decode_layer(): lax.psum_scatter(gate_part, 'tx', scatter_dimension=1, tiled=True)  240 us
    all_gather x1, waiting for transfers between devices, decode_layer(): act_full = lax.all_gather(mlp_act, 'tx', axis=1, tiled=True)  217 us
    reduce_scatter x1, waiting for transfers between devices, decode_layer(): up_sum = lax.psum_scatter(up_part, 'tx', scatter_dimension=1, tiled=True)  189 us
    psum x1, waiting for transfers between devices, decode_layer(): row_stats = lax.psum(row_stats, ('tx', 'tyz'))  152 us
    reduce_scatter x1, waiting for transfers between devices, decode_layer(): lax.psum_scatter(query_part, 'tx', scatter_dimension=0, tiled=True)  92.5 us
    all_gather x1, waiting for transfers between devices, decode_layer(): attended_all = lax.all_gather(attended_heads, 'tx', axis=0, tiled=True)  76.8 us
    reduce_scatter x1, waiting for transfers between devices, decode_layer(): key_rows = lax.psum_scatter(key_part, 'tx', scatter_dimension=0, tiled=True)  72.4 us
    reduce_scatter x1, waiting for transfers between devices, decode_layer(): lax.psum_scatter(block_part.astype(jnp.bfloat16), 'tyz', scatter_dimensio...  37.4 us
  transfers between devices with their start and end apart: 11, of which 10 were waited for; matrix products, arithmetic and copies ran while one was open for 10% of the time, Pallas kernels for 0%

commit v1 on v0

v1 whole, which is shorter than its diff:
```python
import jax
import jax.numpy as jnp
from jax import lax
from jax.sharding import Mesh, PartitionSpec as P

LN_EPS = 1e-5
ROPE_BASE = 10000.0


def rope_rotate(vectors, positions):
    head_dim = vectors.shape[-1]
    half_dim = head_dim // 2
    inv_freq = ROPE_BASE ** (-2.0 * jnp.arange(half_dim, dtype=jnp.float32) / head_dim)
    angles = positions.astype(jnp.float32)[:, None] * inv_freq[None, :]
    bcast_shape = (angles.shape[0],) + (1,) * (vectors.ndim - 2) + (half_dim,)
    cos_part = jnp.cos(angles).reshape(bcast_shape)
    sin_part = jnp.sin(angles).reshape(bcast_shape)
    vec_f32 = vectors.astype(jnp.float32)
    first_half = vec_f32[..., :half_dim]
    second_half = vec_f32[..., half_dim:]
    rotated = jnp.concatenate([first_half * cos_part - second_half * sin_part, second_half * cos_part + first_half * sin_part], axis=-1)
    return rotated.astype(jnp.bfloat16)


def attend_rows(query_rot, key_rot, value_new, k_cache, v_cache, lengths):
    positions = jnp.arange(k_cache.shape[1], dtype=jnp.int32)
    write_mask = (positions[None, :] == lengths[:, None])[:, :, None]
    k_updated = jnp.where(write_mask, key_rot[:, None, :], k_cache)
    v_updated = jnp.where(write_mask, value_new[:, None, :], v_cache)
    scores = jnp.einsum('rhd,rtd->rht', query_rot, k_updated, preferred_element_type=jnp.float32) * (query_rot.shape[-1] ** -0.5)
    valid_mask = (positions[None, :] <= lengths[:, None])[:, None, :]
    scores = jnp.where(valid_mask, scores, -1e30)
    attn_probs = jax.nn.softmax(scores, axis=-1).astype(jnp.bfloat16)
    attended = jnp.einsum('rht,rtd->rhd', attn_probs, v_updated, preferred_element_type=jnp.float32).astype(jnp.bfloat16)
    return attended, k_updated, v_updated


def solution(mesh):
    inner = Mesh(mesh.devices.reshape(4, 4, 4, 2), ('z', 'y', 'x', 'c'))
    f32, bf16 = jnp.float32, jnp.bfloat16

    def decode_layer(residual, ln_scale, w_query, w_key, w_value, w_gate, w_up, w_out, w_down, k_cache, v_cache, lengths):
        feats = residual.shape[1]
        model_dim = feats * 128
        def cols_by_y(w):
            parts = w.reshape(w.shape[0], 4, -1).transpose(1, 0, 2)
            parts = lax.all_to_all(parts, 'y', 0, 0, tiled=True)
            return lax.all_gather(parts, ('z', 'c'), axis=0, tiled=False).reshape((4, 2) + parts.shape)
        wq = lax.all_gather(w_query, ('z', 'c'), axis=0, tiled=False).reshape(4, 2, *w_query.shape)
        wkv = lax.all_gather(jnp.concatenate([w_key, w_value], axis=1), 'z', axis=0, tiled=False)
        wg = cols_by_y(w_gate)
        wu = cols_by_y(w_up)
        wo = lax.all_gather(w_out, ('z', 'c'), axis=0, tiled=False).reshape(4, 2, *w_out.shape)
        wd = lax.all_to_all(w_down.reshape(4, -1, w_down.shape[1]), 'y', 0, 0, tiled=True)
        wd = lax.all_gather(wd, ('z', 'c'), axis=0, tiled=False).reshape((4, 2) + wd.shape)

        rows = residual.reshape(4, 16, 2, 64, feats).transpose(0, 2, 4, 1, 3).reshape(8, feats, 1024)
        scale8 = lax.all_gather(ln_scale, ('z', 'c'), axis=0, tiled=False)
        mine = lax.all_to_all(rows, ('z', 'c'), 0, 0, tiled=True)
        x = mine.astype(f32)
        stats = jnp.stack([jnp.sum(x, axis=(0, 1)), jnp.sum(jnp.square(x), axis=(0, 1))])
        stats = lax.psum(stats, ('y', 'x'))
        mean = stats[0] / model_dim
        var = stats[1] / model_dim - jnp.square(mean)
        hn = ((x - mean) * lax.rsqrt(var + LN_EPS) * scale8.astype(f32)[:, :, None]).astype(bf16)
        hn = lax.all_gather(hn.reshape(8 * feats, 1024), ('y', 'x'), axis=0, tiled=False)
        hn = hn.reshape(4, 4, 4, 2, feats, 1024)
        hn = hn.transpose(2, 0, 1, 3, 4, 5).reshape(4, 4, 8 * feats, 1024)
        hn_y = lax.dynamic_index_in_dim(hn, lax.axis_index('y'), 1, keepdims=False)

        q_part = jnp.einsum('zkr,zckn->rcn', hn_y, wq, preferred_element_type=f32).astype(bf16).reshape(1024, -1)
        kv_part = jnp.einsum('zkr,zkn->rn', hn_y, wkv, preferred_element_type=f32).astype(bf16)
        q_rows = lax.psum_scatter(jnp.concatenate([q_part, kv_part], axis=1), 'y', scatter_dimension=0, tiled=True)
        kv_rows = lax.dynamic_slice_in_dim(q_rows[:, 1280:], lax.axis_index('x') * 64, 64, axis=0)
        q = lax.all_to_all(q_rows[:, :1280].reshape(4, 64, 1280), 'x', 0, 0, tiled=True)
        q = q.transpose(1, 0, 2).reshape(64, 40, 128)
        q_rot = rope_rotate(q, lengths)
        k_rot = rope_rotate(kv_rows[:, :128], lengths)
        o, k_new, v_new = attend_rows(q_rot, k_rot, kv_rows[:, 128:], k_cache, v_cache, lengths)
        o = o.reshape(64, 4, 1280).transpose(1, 0, 2)
        o = lax.all_to_all(o, 'x', 0, 0, tiled=True).reshape(256, 1280)
        o = lax.all_gather(o, 'y', axis=0, tiled=True)

        gate = jnp.einsum('zykr,zcykn->rcn', hn, wg, preferred_element_type=f32).astype(bf16)
        up = jnp.einsum('zykr,zcykn->rcn', hn, wu, preferred_element_type=f32).astype(bf16)
        act = (jax.nn.silu(gate.astype(f32)) * up.astype(f32)).astype(bf16)
        out = jnp.einsum('zcynf,rcn->zyfr', wd, act, preferred_element_type=f32)
        out_o = jnp.einsum('zcnf,rcn->zfr', wo, o.reshape(1024, 2, 640), preferred_element_type=f32)
        here = (jnp.arange(4) == lax.axis_index('y')).astype(f32)[None, :, None, None]
        out = (out + here * out_o[:, None]).astype(bf16)
        out = out.reshape(4, 4, 4, 2 * feats, 1024).transpose(1, 2, 0, 3, 4).reshape(16 * 8 * feats, 1024)
        out = lax.psum_scatter(out, ('y', 'x'), scatter_dimension=0, tiled=True)
        new = (x.reshape(8 * feats, 1024) + out.astype(f32)).astype(bf16).reshape(8, feats, 1024)
        new = lax.all_to_all(new, ('z', 'c'), 0, 0, tiled=True)
        new = new.reshape(4, 2, feats, 16, 64).transpose(0, 3, 1, 4, 2).reshape(8192, feats)
        return new, k_new, v_new

    rc = ('z', 'y', 'x', 'c')
    tx, tyz = ('z', 'y'), ('x', 'c')
    in_specs = (P(None, rc), P(rc), P(tx, tyz), P(tx, None), P(tx, None), P(tx, tyz), P(tx, tyz), P(tyz, tx), P(tyz, tx), P(rc, None, None), P(rc, None, None), P(rc))
    out_specs = (P(None, rc), P(rc, None, None), P(rc, None, None))
    return jax.shard_map(decode_layer, mesh=inner, in_specs=in_specs, out_specs=out_specs, check_vma=False)
```

time: 1330 us -> 700 us (0.53)
  waiting for transfers between devices: 1120 us -> 338 us
  blocking collectives: 14.4 us -> 173 us
  matrix products: 125 us -> 92.3 us
  local copies, waits for them, and re-layouts: 22.5 us -> 51.8 us
    reduce_scatter x6 -> x2, waiting for transfers between devices: 632 us -> 88.8 us  [the longest x1 88.8 us: decode_layer(): out = lax.psum_scatter(out, ('y', 'x'), scatter_dimension=0, tiled=True)]
    psum x1 -> x0, waiting for transfers between devices: 152 us -> none  [decode_layer(): row_stats = lax.psum(row_stats, ('tx', 'tyz'))]
    all_to_all x1 -> x5, blocking collectives: 14.4 us -> 115 us  [the longest x2 66.7 us: cols_by_y(): parts = lax.all_to_all(parts, 'y', 0, 0, tiled=True)]
    all_gather x3 -> x7, waiting for transfers between devices: 329 us -> 242 us  [the longest x2 72.6 us: cols_by_y(): lax.all_gather(parts, ('z', 'c'), axis=0, tiled=False)]
    dot_general x7 -> x6, matrix products: 116 us -> 81.4 us  [the longest x1 22.3 us: decode_layer(): out = jnp.einsum('zcynf,rcn->zyfr', wd, act, preferred_element_type=f32)]
    psum x0 -> x1, blocking collectives: none -> 33.9 us  [decode_layer(): stats = lax.psum(stats, ('y', 'x'))]
    reshape x1 -> x13, local copies, waits for them, and re-layouts: 1.44 us -> 29.3 us  [the longest x1 10.1 us: decode_layer(): out.reshape(4, 4, 4, 2 * feats, 1024).transpose(1, 2, 0, 3, 4)]
    unnamed x0 -> x1, blocking collectives: none -> 13.5 us
  transfers between devices with their start and end apart: 11 -> 11, of which waited for: 10 -> 8; matrix products, arithmetic and copies ran while one was open for 10% -> 13% of each run, Pallas kernels for 0% -> 0%
where the time goes in v1:
time: 700 us; the launch traced here: 691 us
  waiting for transfers between devices  338 us (48%)
  blocking collectives  173 us (25%)
  matrix products  92.3 us (13%)
  local copies, waits for them, and re-layouts  51.8 us (7%)
  between operations  15.4 us (2%)
  starting transfers between devices  11.6 us (2%)
  other arithmetic  8.62 us (1%)
    reduce_scatter x1, waiting for transfers between devices, decode_layer(): out = lax.psum_scatter(out, ('y', 'x'), scatter_dimension=0, tiled=True)  88.8 us
    all_gather x2, waiting for transfers between devices, cols_by_y(): lax.all_gather(parts, ('z', 'c'), axis=0, tiled=False)  72.6 us
    all_gather x1, waiting for transfers between devices, decode_layer(): lax.all_gather(hn.reshape(8 * feats, 1024), ('y', 'x'), axis=0, tiled=False)  72.6 us
    all_to_all x2, blocking collectives, cols_by_y(): parts = lax.all_to_all(parts, 'y', 0, 0, tiled=True)  66.7 us
    all_gather x1, waiting for transfers between devices, decode_layer(): lax.all_gather(wd, ('z', 'c'), axis=0, tiled=False)  60.9 us
    psum x1, blocking collectives, decode_layer(): stats = lax.psum(stats, ('y', 'x'))  33.9 us
    dot_general x1, matrix products, decode_layer(): out = jnp.einsum('zcynf,rcn->zyfr', wd, act, preferred_element_type=f32)  22.3 us
    dot_general x1, matrix products, decode_layer(): jnp.einsum('zykr,zcykn->rcn', hn, wu, preferred_element_type=f32)  20.8 us
  transfers between devices with their start and end apart: 11, of which 8 were waited for; matrix products, arithmetic and copies ran while one was open for 13% of the time, Pallas kernels for 0%

profile of v1, /device:TPU:1, one launch (start us, length us, event | category | flops | bytes accessed | tf_op | source)
XLA Modules:
  0.0 690.9 jit_solution(3195166187045520449)
XLA Ops:
  12.2 6.9 %all-to-all-start = ((bf16[8,40,1024]{2,1,0:T(8,128)(2,1)}), bf16[8,40,1024]{2,1,0:T(8,128)(2,1)S(1)}, u32[]{:S(2)}, u32[]{:S(2)}) async-start(bf16[8,40,1024]{2,1,0:T(8,128)(2,1)} %reshape.213), calls=%async_computation | async-start | bytes 1310720 | tf_op jit(solution)/shard_map/all_to_all | solution.py:59
  20.7 13.5 %all-reduce = bf16[320]{0:T(512)(128)(2,1)S(1)} all-reduce(bf16[320]{0:T(512)(128)(2,1)S(1)} %dynamic-update-slice), channel_id=2, replica_groups=mesh['z'=4,'y'=4,'x'=4,'c'=2] {'z','c'}, use_global_device_ids=true, to_apply=%add | all-reduce | flops 320 | bytes 1280
  34.6 33.9 %psum.7 = f32[2,1024]{1,0:T(2,128)S(1)} all-reduce(f32[2,1024]{1,0:T(2,128)S(1)} %pad_maximum_fusion.3), channel_id=1, replica_groups=mesh['z'=4,'y'=4,'x'=4,'c'=2] {'y','x'}, use_global_device_ids=true, to_apply=%region_2.0 | all-reduce | flops 2048 | bytes 16384 | tf_op jit(solution)/shard_map/psum | solution.py:62
  70.5 10.7 %all-gather.5 = bf16[1280,256]{1,0:T(8,128)(2,1)S(1)} all-gather(bf16[320,256]{1,0:T(8,128)(2,1)S(1)} %pad_maximum_fusion.1), channel_id=7, replica_groups=mesh['z'=4,'y'=4,'x'=4,'c'=2] {'z'}, dimensions={0}, use_global_device_ids=true | all-gather | bytes 819200 | tf_op jit(solution)/shard_map/all_gather | solution.py:50
  81.1 72.6 %all-gather.15.cloned.1.call-done = bf16[16,320,1024]{2,1,0:T(8,128)(2,1)} async-done(((bf16[1,320,1024]{2,1,0:T(8,128)(2,1)}), bf16[16,320,1024]{2,1,0:T(8,128)(2,1)}) %all-gather.15.cloned.1.call-update) | async-done | bytes 10485776 | tf_op jit(solution)/shard_map/all_gather | solution.py:66
  153.7 10.2 %copy.85 = bf16[4,4,4,2,40,1024]{5,4,3,2,0,1:T(8,128)(2,1)} copy(bf16[4,4,4,2,40,1024]{5,4,3,0,2,1:T(8,128)(2,1)} %bitcast.134) | data formatting | bytes 20971520 | tf_op jit(solution)/shard_map/transpose | solution.py:68
  163.9 20.1 %all-gather.25.cloned.1.call-done = bf16[2560,640]{1,0:T(8,128)(2,1)} async-done(((bf16[320,640]{1,0:T(8,128)(2,1)}), bf16[2560,640]{1,0:T(8,128)(2,1)}) %all-gather.25.cloned.1.call-update) | async-done | bytes 3276816 | tf_op jit(solution)/shard_map/all_gather | solution.py:49
  184.0 7.8 %bitcast_convert_fusion = bf16[1024,2,640]{0,2,1:T(8,128)(2,1)} fusion(bf16[4,2,320,640]{3,2,1,0:T(8,128)(2,1)} %bitcast.157, bf16[4,4,320,1024]{3,2,0,1:T(8,128)(2,1)} %bitcast.130, s32[]{:T(128)S(6)} %select_n.18), kind=kOutput, calls=%fused_computation.13 | convolution fusion | flops 3356753920 | bytes 8519684 | tf_op jit(solution)/shard_map/zkr,zckn->rcn/dot_general | solution.py:71
  201.6 39.8 %all_to_all.35 = bf16[4,320,640]{2,1,0:T(8,128)(2,1)} all-to-all(bf16[4,320,640]{2,1,0:T(8,128)(2,1)S(1)} %copy.86), channel_id=1, replica_groups=mesh['z'=4,'y'=4,'x'=4,'c'=2] {'y'}, dimensions={0} | all-to-all | bytes 3276800 | tf_op jit(solution)/shard_map/all_to_all | solution.py:47
  242.3 26.9 %all_to_all.36 = bf16[4,320,640]{2,1,0:T(8,128)(2,1)} all-to-all(bf16[4,320,640]{2,1,0:T(8,128)(2,1)S(1)} %copy.88), channel_id=1, replica_groups=mesh['z'=4,'y'=4,'x'=4,'c'=2] {'y'}, dimensions={0} | all-to-all | bytes 3276800 | tf_op jit(solution)/shard_map/all_to_all | solution.py:47
  298.2 10.8 %all_to_all.37 = bf16[4,64,1280]{2,1,0:T(8,128)(2,1)} all-to-all(bf16[4,64,1280]{2,1,0:T(8,128)(2,1)S(1)} %bitcast.145), channel_id=1, replica_groups=mesh['z'=4,'y'=4,'x'=4,'c'=2] {'x'}, dimensions={0} | all-to-all | bytes 1310720 | tf_op jit(solution)/shard_map/all_to_all | solution.py:81
  309.2 20.6 %all_to_all.38 = bf16[4,640,320]{1,2,0:T(8,128)(2,1)} all-to-all(bf16[4,640,320]{1,2,0:T(8,128)(2,1)S(1)} %bitcast.138), channel_id=1, replica_groups=mesh['z'=4,'y'=4,'x'=4,'c'=2] {'y'}, dimensions={0} | all-to-all | bytes 3276800 | tf_op jit(solution)/shard_map/all_to_all | solution.py:54
  330.1 7.3 %reshape.229 = bf16[4,2,640,320]{2,1,0,3:T(2,128)(2,1)S(1)} reshape(bf16[5120,320]{0,1:T(8,128)(2,1)} %all-gather.27.cloned.1.call-done) | data formatting | bytes 6553600 | tf_op jit(solution)/shard_map/reshape | solution.py:53
  337.4 21.8 %all-gather.19.cloned.1.call-done = bf16[32,320,640]{2,1,0:T(8,128)(2,1)} async-done(((bf16[4,320,640]{2,1,0:T(8,128)(2,1)}), bf16[32,320,640]{2,1,0:T(8,128)(2,1)}) %all-gather.19.cloned.1.call-update) | async-done | bytes 13107216 | tf_op jit(solution)/shard_map/all_gather | solution.py:48
  359.2 20.8 %fusion.4 = bf16[1024,2,640,1,1]{2,0,4,1,3:T(8,128)(2,1)} fusion(bf16[4,4,320,1024,1]{3,2,0,4,1:T(8,128)(2,1)} %bitcast.132, bf16[4,2,4,320,640]{4,3,2,1,0:T(8,128)(2,1)} %bitcast.154), kind=kOutput, calls=%fused_computation.5 | convolution fusion | flops 13421772800 | bytes 26214400 | tf_op jit(solution)/shard_map/zykr,zcykn->rcn/dot_general | solution.py:84
  380.0 50.8 %all-gather.21.cloned.1.call-done = bf16[32,320,640]{2,1,0:T(8,128)(2,1)} async-done(((bf16[4,320,640]{2,1,0:T(8,128)(2,1)}), bf16[32,320,640]{2,1,0:T(8,128)(2,1)}) %all-gather.21.cloned.1.call-update) | async-done | bytes 13107216 | tf_op jit(solution)/shard_map/all_gather | solution.py:48
  430.9 20.8 %fusion.2 = bf16[1024,2,640,1,1]{2,0,4,1,3:T(8,128)(2,1)} fusion(bf16[4,4,320,1024,1]{3,2,0,4,1:T(8,128)(2,1)} %bitcast.133, bf16[4,2,4,320,640]{4,3,2,1,0:T(8,128)(2,1)} %bitcast.155), kind=kOutput, calls=%fused_computation.3 | convolution fusion | flops 13421772800 | bytes 26214400 | tf_op jit(solution)/shard_map/zykr,zcykn->rcn/dot_general | solution.py:85
  451.7 15.3 %all-gather.17.cloned.1.call-done = bf16[1024,1280]{1,0:T(8,128)(2,1)} async-done(((bf16[256,1280]{1,0:T(8,128)(2,1)}), bf16[1024,1280]{1,0:T(8,128)(2,1)}) %all-gather.17.cloned.1.call-update) | async-done | bytes 2621456 | tf_op jit(solution)/shard_map/all_gather | solution.py:82
  471.5 7.0 %fusion.19 = f32[4,320,1024]{2,1,0:T(8,128)} fusion(bf16[1024,2,640,1]{0,2,1,3:T(8,128)(2,1)} %bitcast.142, bf16[4,2,640,320]{2,1,0,3:T(2,128)(2,1)S(1)} %reshape.229), kind=kOutput, calls=%fused_computation.25 | convolution fusion | flops 3355443200 | bytes 11141120 | tf_op jit(solution)/shard_map/zcnf,rcn->zfr/dot_general | solution.py:88
  478.5 60.9 %all-gather.23.cloned.1.call-done = bf16[32,640,320]{1,2,0:T(8,128)(2,1)} async-done(((bf16[4,640,320]{1,2,0:T(8,128)(2,1)}), bf16[32,640,320]{1,2,0:T(8,128)(2,1)}) %all-gather.23.cloned.1.call-update) | async-done | bytes 13107216 | tf_op jit(solution)/shard_map/all_gather | solution.py:55
  539.4 22.3 %fusion.1 = bf16[4,4,320,1024]{3,2,1,0:T(8,128)(2,1)} fusion(f32[4,320,1024]{2,1,0:T(8,128)} %fusion.19, f32[4]{0:T(128)S(1)} %compare_convert_fusion, bf16[4,2,4,640,320]{3,4,2,1,0:T(8,128)(2,1)} %bitcast.156, bf16[1024,2,640,1,1]{2,0,4,1,3:T(8,128)(2,1)} %fusion.4, bf16[1024,2,640,1,1]{2,0,4,1,3:T(8,128)(2,1)} %fusion.2), kind=kOutput, calls=%fused_computation.2 | convolution fusion | flops 13447987200 | bytes 34078736 | tf_op jit(solution)/shard_map/zcynf,rcn->zyfr/dot_general | solution.py:87
  561.7 10.1 %copy.100 = bf16[4,4,4,80,1024]{4,3,0,2,1:T(8,128)(2,1)} copy(bf16[4,4,4,80,1024]{4,3,2,1,0:T(8,128)(2,1)} %bitcast.135) | data formatting | bytes 20971520 | tf_op jit(solution)/shard_map/reshape | solution.py:91
  571.8 88.8 %reduce-scatter.5.cloned.1.call-done = bf16[320,1024]{1,0:T(8,128)(2,1)} async-done(((bf16[5120,1024]{1,0:T(8,128)(2,1)}), bf16[320,1024]{1,0:T(8,128)(2,1)}) %reduce-scatter.5.cloned.1.call-update) | async-done | bytes 655376 | tf_op jit(solution)/shard_map/reduce_scatter | solution.py:92
  662.0 17.2 %all_to_all.39 = bf16[8,40,1024]{2,1,0:T(8,128)(2,1)S(1)} all-to-all(bf16[8,40,1024]{2,1,0:T(8,128)(2,1)S(1)} %bitcast.146), channel_id=1, replica_groups=mesh['z'=4,'y'=4,'x'=4,'c'=2] {'z','c'}, dimensions={0} | all-to-all | bytes 1310720 | tf_op jit(solution)/shard_map/all_to_all | solution.py:94
  (98 shorter events, 58.4 us)
Async XLA Ops:
  10.3 8.9 %copy-start.13 = (u32[128]{0:T(128)S(1)}, u32[128]{0:T(128)}, u32[]{:S(2)}) copy-start(u32[128]{0:T(128)} %constant.52) | copy-start | bytes 1540
  10.3 10.1 %copy-start.12 = (bf16[40]{0:T(256)(128)(2,1)S(1)}, bf16[40]{0:T(256)(128)(2,1)}, u32[]{:S(2)}) copy-start(bf16[40]{0:T(256)(128)(2,1)} %param.13) | copy-start | bytes 244
  12.2 58.2 %copy-start.9 = (bf16[320,128]{1,0:T(8,128)(2,1)S(1)}, bf16[320,128]{1,0:T(8,128)(2,1)}, u32[]{:S(2)}) copy-start(bf16[320,128]{1,0:T(8,128)(2,1)} %param.16) | copy-start | bytes 245764
  12.2 58.2 %copy-start.10 = (bf16[320,128]{1,0:T(8,128)(2,1)S(1)}, bf16[320,128]{1,0:T(8,128)(2,1)}, u32[]{:S(2)}) copy-start(bf16[320,128]{1,0:T(8,128)(2,1)} %param.15) | copy-start | bytes 245764
  12.2 22.1 %all-to-all-start = ((bf16[8,40,1024]{2,1,0:T(8,128)(2,1)}), bf16[8,40,1024]{2,1,0:T(8,128)(2,1)S(1)}, u32[]{:S(2)}, u32[]{:S(2)}) async-start(bf16[8,40,1024]{2,1,0:T(8,128)(2,1)} %reshape.213), calls=%async_computation | async-start | bytes 1310720 | tf_op jit(solution)/shard_map/all_to_all | solution.py:59
  19.2 134.5 %all-gather.15.cloned.1.call-start = ((), (), s32[]{:S(2)}) async-start(), calls=%async_computation.9 | async-start | bytes 11141120 | tf_op jit(solution)/shard_map/all_gather | solution.py:66
  34.3 129.6 %copy-start = (bf16[8,40,1024]{2,1,0:T(8,128)(2,1)}, bf16[8,40,1024]{2,1,0:T(8,128)(2,1)S(1)}, u32[]{:S(2)}) copy-start(bf16[8,40,1024]{2,1,0:T(8,128)(2,1)S(1)} %all-to-all-done) | copy-start | bytes 1966084
  69.6 114.4 %all-gather.25.cloned.1.call-start = ((), (), s32[]{:S(2)}) async-start(), calls=%async_computation.16 | async-start | bytes 3686400 | tf_op jit(solution)/shard_map/all_gather | solution.py:49
  70.4 199.0 %reduce-scatter.3.cloned.1.call-start = ((), (), s32[]{:S(2)}) async-start(), calls=%async_computation.10 | async-start | bytes 3932160 | tf_op jit(solution)/shard_map/reduce_scatter | solution.py:73
  199.6 130.5 %all-gather.27.cloned.1.call-start = ((), (), s32[]{:S(2)}) async-start(), calls=%async_computation.17 | async-start | bytes 3686400 | tf_op jit(solution)/shard_map/all_gather | solution.py:53
  200.2 159.1 %all-gather.19.cloned.1.call-start = ((), (), s32[]{:S(2)}) async-start(), calls=%async_computation.13 | async-start | bytes 14745600 | tf_op jit(solution)/shard_map/all_gather | solution.py:48
  201.6 40.0 %copy-start.5 = (bf16[320,2560]{1,0:T(8,128)(2,1)S(1)}, bf16[320,2560]{1,0:T(8,128)(2,1)}, u32[]{:S(2)}) copy-start(bf16[320,2560]{1,0:T(8,128)(2,1)} %param.18) | copy-start | bytes 4915204
  241.4 189.4 %all-gather.21.cloned.1.call-start = ((), (), s32[]{:S(2)}) async-start(), calls=%async_computation.14 | async-start | bytes 14745600 | tf_op jit(solution)/shard_map/all_gather | solution.py:48
  242.3 26.9 %copy-start.11 = (s32[64]{0:T(128)S(1)}, s32[64]{0:T(128)}, u32[]{:S(2)}) copy-start(s32[64]{0:T(128)} %param.23) | copy-start | bytes 772
  269.2 6.6 copy-start.7
  269.2 6.6 copy-start.8
  269.4 6.1 slice-start
  271.5 12.6 %all-to-all-start.4 = ((bf16[4,64,1280]{2,1,0:T(8,128)(2,1)}), bf16[4,64,1280]{2,1,0:T(8,128)(2,1)S(1)}, u32[]{:S(2)}, u32[]{:S(2)}) async-start(bf16[4,64,1280]{2,1,0:T(8,128)(2,1)} %bitcast.37), calls=%async_computation.5 | async-start | bytes 1310720 | tf_op jit(solution)/shard_map/all_to_all | solution.py:75
  275.4 191.5 %all-gather.17.cloned.1.call-start = ((), (), s32[]{:S(2)}) async-start(), calls=%async_computation.11 | async-start | bytes 3276800 | tf_op jit(solution)/shard_map/all_gather | solution.py:82
  286.9 2.4 copy-start.3
  297.9 11.2 %copy-start.6 = (bf16[2560,320]{0,1:T(8,128)(2,1)S(1)}, bf16[2560,320]{0,1:T(8,128)(2,1)}, u32[]{:S(2)}) copy-start(bf16[2560,320]{0,1:T(8,128)(2,1)} %param.20) | copy-start | bytes 4915204
  309.0 230.3 %all-gather.23.cloned.1.call-start = ((), (), s32[]{:S(2)}) async-start(), calls=%async_computation.15 | async-start | bytes 14745600 | tf_op jit(solution)/shard_map/all_gather | solution.py:55
  329.8 330.8 %reduce-scatter.5.cloned.1.call-start = ((), (), s32[]{:S(2)}) async-start(), calls=%async_computation.12 | async-start | bytes 11141120 | tf_op jit(solution)/shard_map/reduce_scatter | solution.py:92
  571.8 88.8 %copy-start.1 = (bf16[8,40,1024]{2,1,0:T(8,128)(2,1)S(1)}, bf16[8,40,1024]{2,1,0:T(8,128)(2,1)}, u32[]{:S(2)}) copy-start(bf16[8,40,1024]{2,1,0:T(8,128)(2,1)} %copy-done) | copy-start | bytes 1966084
  (2 other events, 2.8 us)
Sparse Core Ops, SparseCore 0:
  69.7 83.9 all-gather.14
  155.4 28.5 all-gather.24
  199.7 56.3 reduce-scatter.2
  257.6 30.4 all-gather.26
  289.7 69.5 all-gather.18
  360.8 70.0 all-gather.20
  432.5 34.4 all-gather.16
  468.7 70.6 all-gather.22
  571.9 88.6 reduce-scatter.4

commit v2 on v0

v2 whole, which is shorter than its diff:
```python
import jax
import jax.numpy as jnp
from jax import lax
from jax.experimental import pallas as pl
from jax.experimental.pallas import tpu as pltpu
from jax.sharding import Mesh, PartitionSpec as P

LN_EPS = 1e-5
ROPE_BASE = 10000.0
MESH = pl.DeviceIdType.MESH
DMA = pltpu.SemaphoreType.DMA
F32, BF16 = jnp.float32, jnp.bfloat16
ROWS, MODEL, FEATS, BATCH = 1024, 5120, 40, 8192
KB, NB, HB, QB, HD, SUB = 1280, 640, 320, 896, 128, 80
MINE, SEQ, HEADS, LANE = 64, 64, 40, 128
NR, NC, NJ, NG = 4, 2, 16, 8
SPLIT = 384
CUT = 512
TILE = 256
RING = range(4)
AWAY = (1, 3, 2)
GROUPS = ((0, 1), (1, 2), (2, 4))
ORDER = (0, 1, 3, 2)
PAIRS = tuple(sorted(((dy, dx) for dy in RING for dx in RING if dy or dx), key=lambda p: (p.count(2), sum(p))))
NT = (((1,), (1,)), ((), ()))


def flip(i, d):
    return (i, i + 1 - 2 * lax.rem(i, 2), lax.rem(i + 2, 4), 3 - i)[d]


def put(src, dst, ssem, rsem, dev):
    pltpu.make_async_remote_copy(src_ref=src, dst_ref=dst, send_sem=ssem, recv_sem=rsem, device_id=dev, device_id_type=MESH).start()


def three(ref):
    return sum(ref[k].astype(F32) for k in range(3))


def get(src, dst, sem):
    pltpu.make_async_copy(src, dst, sem).start()


def first(n):
    return pl.ds(0, n)


def drain(ref, sem):
    pltpu.make_async_copy(ref, ref, sem).wait()


class Wide:
    def __init__(self, land, src, sems, pos):
        self.land, self.src = land, src
        self.send, self.yr, self.zr, self.fr, self.dr, self.loc = sems
        self.z, self.y, self.x, self.c = pos
        self.base = self.c * 16

    def piece(self, yy):
        return self.src.at[:, pl.ds(pl.multiple_of(yy * NB, LANE), NB)]

    def at(self, dz, g, base=None):
        lo, hi = GROUPS[g]
        return self.land.at[pl.ds((self.base if base is None else base) + dz * 4 + lo, hi - lo)]

    def start_local(self):
        get(self.piece(self.y), self.land.at[self.base], self.loc)

    def y_send(self):
        for dy in AWAY:
            yy = flip(self.y, dy)
            put(self.piece(yy), self.land.at[self.base + dy], self.send, self.yr.at[dy - 1], dict(y=yy))

    def z_send(self, g):
        if g:
            for dy in range(*GROUPS[g]):
                drain(self.land.at[self.base + dy], self.yr.at[dy - 1])
        for k, dz in enumerate(AWAY[:2]):
            to = dict(z=flip(self.z, dz))
            if g:
                put(self.at(0, g), self.at(dz, g), self.send, self.zr.at[k * 3 + g], to)
            else:
                put(self.piece(self.y), self.land.at[self.base + dz * 4], self.send, self.zr.at[k * 3], to)
        self.d2d(0, g)

    def forward(self, g):
        for k, dz in enumerate(AWAY[:2]):
            drain(self.at(dz, g), self.zr.at[k * 3 + g])
        src, to = (1, 3) if g < 2 else (3, 1)
        put(self.at(src, g), self.at(2, g), self.send, self.fr.at[g], dict(z=flip(self.z, to)))
        self.d2d(1, g)
        self.d2d(3, g)

    def last(self, g):
        drain(self.at(2, g), self.fr.at[g])
        self.d2d(2, g)

    def d2d(self, dz, g):
        to = dict(c=1 - self.c)
        if dz or g:
            put(self.at(dz, g), self.at(dz, g), self.send, self.dr.at[dz * 3 + g], to)
        else:
            put(self.piece(self.y), self.land.at[self.base], self.send, self.dr.at[0], to)

    def load(self, dz, tile, sem):
        if dz == 0:
            drain(self.land.at[self.base], self.loc)
        for g in range(3):
            drain(self.at(dz, g, 16 - self.base), self.dr.at[dz * 3 + g])
        for cc in range(NC):
            get(self.land.at[pl.ds(cc * 16 + dz * 4, 4)], tile.at[:, :, pl.ds(cc * NB, NB)], sem)

    def finish(self):
        drain(self.land.at[first(31)], self.send)


class Narrow:
    def __init__(self, land, parts, sems, pos):
        self.land, self.parts = land, parts
        self.send, self.yr, self.zr, self.fr, self.dr, self.loc = sems
        self.z, self.y, self.x, self.c = pos
        self.s = lax.rem(self.c + self.y, 2)

    def own(self, slot):
        lo = 0
        for ref in self.parts:
            hi = lo + ref.shape[1]
            yield ref, self.land.at[slot, :, pl.ds(lo, hi - lo)]
            lo = hi

    def start(self):
        @pl.when(self.s == 0)
        def _():
            for src, dst in self.own(0):
                get(src, dst, self.loc)

        @pl.when(self.s == 1)
        def _():
            for src, dst in self.own(1):
                put(src, dst, self.send, self.yr, dict(y=flip(self.y, 1), c=1 - self.c))

    def z_first(self):
        @pl.when(self.s == 0)
        def _():
            for k, dz in enumerate(AWAY[:2]):
                for (src, _), (_, dst) in zip(self.own(0), self.own(dz * 2)):
                    put(src, dst, self.send, self.zr.at[k], dict(z=flip(self.z, dz)))
            for src, dst in self.own(0):
                put(src, dst, self.send, self.dr.at[0], dict(c=1 - self.c))

    def z_second(self):
        @pl.when(self.s == 1)
        def _():
            src = self.land.at[1]
            drain(src, self.yr)
            for k, dz in enumerate(AWAY[:2]):
                put(src, self.land.at[dz * 2 + 1], self.send, self.zr.at[k], dict(z=flip(self.z, dz)))
            put(src, src, self.send, self.dr.at[0], dict(c=1 - self.c))

    def half(self, slot, k):
        return self.land.at[slot, pl.ds(k * HB // 2, HB // 2)]

    def forward(self):
        for k, dz in enumerate(AWAY[:2]):
            slot = dz * 2 + self.s
            piece = self.land.at[slot]
            drain(piece, self.zr.at[k])
            put(self.half(slot, k), self.half(4 + self.s, k), self.send, self.fr.at[k], dict(z=flip(self.z, AWAY[1 - k])))
            put(piece, piece, self.send, self.dr.at[1 + k], dict(c=1 - self.c))

    def last(self):
        for k in range(NC):
            piece = self.half(4 + self.s, k)
            drain(piece, self.fr.at[k])
            put(piece, piece, self.send, self.dr.at[3 + k], dict(c=1 - self.c))

    def load(self, dz, tile, sem):
        o = 1 - self.s
        if dz == 0:
            @pl.when(self.s == 0)
            def _():
                drain(self.land.at[0], self.loc)
        if dz == 2:
            for k in range(NC):
                drain(self.half(4 + o, k), self.dr.at[3 + k])
        else:
            drain(self.land.at[dz * 2 + o], self.dr.at[(dz + 1) // 2])
        get(self.land.at[pl.ds(dz * 2, 2)], tile, sem)

    def finish(self):
        for s in range(NC):
            @pl.when(self.s == s)
            def _():
                drain(self.land.at[first(7 + s)], self.send)


WIDE_SEMS = [DMA, DMA((3,)), DMA((6,)), DMA((3,)), DMA((12,)), DMA]
NARROW_SEMS = [DMA, DMA, DMA((2,)), DMA((2,)), DMA((5,)), DMA]
HBM_BUFS = dict(
    Q=((NG, HB, QB), BF16), G=((NG * NR, HB, NB), BF16), U=((NG * NR, HB, NB), BF16), D=((NG * NR, HB, NB), BF16), O=((NG, HB, NB), BF16),
    hnT=((NR, NR, HB, ROWS), BF16), a1=((NR, NR - 1, HB, CUT), BF16), b1=((NR, NR - 1, NR, SUB, ROWS - CUT), BF16))
VMEM_BUFS = dict(
    rT=((FEATS, BATCH), BF16), xs=((NG, FEATS, ROWS + LANE), BF16), F=((NG, FEATS, ROWS + LANE), BF16), S=((NJ, 2, ROWS), F32),
    hs=((NR, SUB, ROWS), BF16), hn=((NR, ROWS, KB), BF16), wt=((NC, NR, HB, KB), BF16), wo_t=((NC, NC, HB, NB), BF16),
    gacc=((ROWS, KB), F32), uacc=((ROWS, KB), F32), qout=((NJ, MINE, QB), BF16), q_in=((NJ, MINE, NB), BF16), kv_in=((NC, MINE, 2 * HD), BF16),
    q3=((MINE * HEADS, HD), F32), lenb=((MINE, HD), F32), kc=((MINE, SEQ, HD), BF16), vc=((MINE, SEQ, HD), BF16), kn=((MINE, 2 * HD), F32),
    o_v=((MINE, MODEL), BF16), o_in=((NJ, MINE, NB), BF16), act=((ROWS, KB), BF16), sb=((NC, NR, HB, ROWS), BF16),
    va=((NR - 1, HB, CUT), BF16), vb=((NR - 1, NR, SUB, ROWS - CUT), BF16), s2a=((NR, HB, CUT), BF16), s2b=((NR, NR, SUB, ROWS - CUT), BF16),
    a2=((NR, NR - 1, SUB, CUT), BF16), b2=((NR, NR - 1, SUB, ROWS - CUT), BF16), fs=((NR, NC, FEATS, ROWS), BF16), fin=((NG, FEATS, ROWS), BF16), ov=((FEATS, BATCH), BF16))
ONE, EACH, BY_GROUP = (), (NR,), (NG,)
SEMS = dict(f_s=ONE, s_s=ONE, s_r=ONE, own_l=ONE, q_s=ONE, q_r=ONE, kv_s=ONE, kv_r=ONE, o_s=ONE, o_r=ONE, fin_s=ONE, out_l=ONE,
            a1s=EACH, a1r=EACH, b1s=EACH, b1r=EACH, a2s=EACH, a2r=EACH, b2s=EACH, b2r=EACH, ag_s=EACH, ag_r=EACH, ld=EACH, wsem=EACH, osem=EACH, vsem=EACH,
            f_r=BY_GROUP, fin_r=BY_GROUP)


def kernel(res, ls, lens, wq, wk, wv, wg, wu, wdT, woT, kc_h, vc_h, outT, kc_o, vc_o, *rest):
    rest = list(rest)

    class b:
        pass
    for name in list(HBM_BUFS) + list(VMEM_BUFS) + list(SEMS):
        setattr(b, name, rest.pop(0))
    pos = z, y, x, c = tuple(lax.axis_index(a) for a in 'zyxc')
    flow = lambda kind, land, src: kind(land, src, [rest.pop(0) for _ in WIDE_SEMS], pos)
    fq = flow(Narrow, b.Q, (wq, wk, wv))
    fg, fu, fd = flow(Wide, b.G, wg), flow(Wide, b.U, wu), flow(Wide, b.D, wdT)
    fo = flow(Narrow, b.O, (woT,))
    me = y * 4 + x
    row_low = lax.broadcasted_iota(jnp.int32, (FEATS, LANE), 1) < LANE // 2

    bar = pltpu.get_barrier_semaphore()
    peers = [dict(z=flip(z, dz), c=cc) for dz in AWAY for cc in (c, 1 - c)] + [dict(c=1 - c), dict(y=flip(y, 1), c=1 - c)]
    peers += [dict(y=flip(y, dy), x=flip(x, dx)) for dy, dx in PAIRS]
    for p in peers:
        pl.semaphore_signal(bar, inc=1, device_id=p, device_id_type=MESH)
    get(res, b.rT, b.ld.at[0])
    get(kc_h, b.kc, b.ld.at[1])
    get(vc_h, b.vc, b.ld.at[2])
    for f in (fg, fu, fd):
        f.start_local()
    pl.semaphore_wait(bar, len(peers))
    fq.start()
    fo_start = fo.start

    drain(b.rT, b.ld.at[0])
    scale = jnp.broadcast_to(ls[...].astype(F32), (LANE, FEATS)).T.astype(BF16)
    for dz in AWAY + (0,):
        zz = flip(z, dz)
        for p in range(NG):
            pair = b.rT[:, pl.ds(pl.multiple_of(zz * 2 * ROWS + p * 2 * LANE, LANE), 2 * LANE)].astype(F32)
            t0, t1 = pair[:, :LANE], pair[:, LANE:]
            at = pl.ds(p * LANE, LANE)
            b.xs[dz * 2, :, at] = jnp.where(row_low, t0, pltpu.roll(t1, LANE // 2, 1)).astype(BF16)
            b.xs[dz * 2 + 1, :, at] = jnp.where(row_low, pltpu.roll(t0, LANE // 2, 1), t1).astype(BF16)
        for cc in range(NC):
            b.xs[dz * 2 + cc, :, ROWS:] = scale
        for cc in (c, 1 - c)[dz == 0:]:
            put(b.xs.at[dz * 2 + cc], b.F.at[dz * 2 + c], b.f_s, b.f_r.at[dz * 2 + c], dict(z=flip(z, dz), c=cc))
    b.F[c] = b.xs[c]
    fq.z_first()
    fg.z_send(0)
    fu.z_send(0)

    for dz in RING:
        for cc in (c, 1 - c)[dz == 0:]:
            drain(b.F.at[dz * 2 + cc], b.f_r.at[dz * 2 + cc])
    tot = sq = jnp.zeros((FEATS, ROWS), F32)
    for i in range(NG):
        v = b.F[i, :, :ROWS].astype(F32)
        tot, sq = tot + v, sq + v * v
    b.S[me] = jnp.concatenate([jnp.sum(v, axis=0, keepdims=True) for v in (tot, sq)], axis=0)
    for dy, dx in PAIRS:
        put(b.S.at[me], b.S.at[me], b.s_s, b.s_r, dict(y=flip(y, dy), x=flip(x, dx)))
    drain(b.S.at[first(NJ - 1)], b.s_r)
    stats = sum(b.S[i] for i in range(NJ)) / MODEL
    mean = stats[0:1]
    inv = lax.rsqrt(stats[1:2] - mean * mean + LN_EPS)
    for dz in RING:
        both = []
        for cc in range(NC):
            i = dz * 2 + cc
            both.append((b.F[i, :, :ROWS].astype(F32) - mean) * inv * b.F[i, :, ROWS:].astype(F32)[:, 0:1])
        b.hs[dz] = jnp.concatenate(both, axis=0).astype(BF16)

    mine = lambda d: pl.ds(pl.multiple_of(flip(x, d) * SUB, 16), SUB)
    A, B = first(SPLIT), pl.ds(SPLIT, ROWS - SPLIT)
    get(b.hs, b.hnT.at[:, 0, mine(0)], b.own_l)
    for d in AWAY:
        put(b.hs.at[:, :, A], b.hnT.at[:, 0, mine(0), A], b.ag_s.at[0], b.ag_r.at[0], dict(x=flip(x, d)))
        put(b.hs.at[:, :, B], b.hnT.at[:, d, mine(0), B], b.ag_s.at[1], b.ag_r.at[1], dict(y=flip(y, d)))
    fg.y_send()
    fq.z_second()
    part_a = lambda n: b.hnT.at[:, 0, first(n * SUB), A]
    part_b = lambda n: b.hnT.at[:, first(n), first(SUB), B]
    drain(b.hnT.at[:, 0, mine(0)], b.own_l)
    drain(part_a(3), b.ag_r.at[0])
    for d in AWAY:
        put(b.hnT.at[:, 0, :, A], b.hnT.at[:, d, :, A], b.ag_s.at[2], b.ag_r.at[2], dict(y=flip(y, d)))
    drain(part_b(3), b.ag_r.at[1])
    for d in AWAY:
        put(b.hnT.at[:, :, mine(0), B], b.hnT.at[:, :, mine(0), B], b.ag_s.at[3], b.ag_r.at[3], dict(x=flip(x, d)))
    all_a = b.hnT.at[:, first(3), :, A]
    all_b = b.hnT.at[:, :, first((NR - 1) * SUB), B]
    fu.y_send()
    fo_start()
    fd.y_send()
    fq.forward()
    fg.forward(0)
    fu.forward(0)
    fg.z_send(1)
    fg.z_send(2)
    fq.last()
    fd.z_send(0)
    fg.forward(1)
    fg.forward(2)
    fg.last(0)
    fu.last(0)

    drain(all_a, b.ag_r.at[2])
    drain(all_b, b.ag_r.at[3])

    def load_hn(dz, slot):
        get(b.hnT.at[dz], b.wt.at[slot, :, :, first(ROWS)], b.wsem.at[slot])

    def turn_hn(dz, slot):
        drain(b.wt.at[slot, :, :, first(ROWS)], b.wsem.at[slot])

        @pl.loop(0, ROWS // LANE)
        def _(r):
            at = pl.ds(pl.multiple_of(r * LANE, LANE), LANE)
            b.hn[dz, at, :] = b.wt[slot, :, :, at].reshape(KB, LANE).T

    load_hn(0, 0)
    for dz in RING:
        if dz < 3:
            load_hn(dz + 1, (dz + 1) % 2)
        turn_hn(dz, dz % 2)

    def load_q(i):
        fq.load(ORDER[i], b.wt.at[i % 2, first(2), :, first(QB)], b.wsem.at[i % 2])

    load_q(0)
    for i, dz in enumerate(ORDER):
        if i < 3:
            load_q(i + 1)
        w_at = (i % 2, first(2), slice(None), first(QB))
        drain(b.wt.at[w_at], b.wsem.at[i % 2])

        @pl.loop(0, ROWS // TILE)
        def _(r):
            at = pl.ds(pl.multiple_of(r * TILE, TILE), TILE)
            new = jnp.dot(b.hn[dz, at, :NB], b.wt[w_at].reshape(NB, QB), preferred_element_type=F32)
            if i:
                new += b.gacc[at, :QB]
            if i < 3:
                b.gacc[at, :QB] = new
            else:
                b.qout[pl.ds(r * 4, 4)] = new.astype(BF16).reshape(4, MINE, QB)
    for dy, dx in PAIRS:
        yy, xx = flip(y, dy), flip(x, dx)
        put(b.qout.at[yy * 4 + xx, :, first(NB)], b.q_in.at[me], b.q_s, b.q_r, dict(y=yy, x=xx))
    put(b.qout.at[flip(y, 2) * 4 + x, :, pl.ds(NB, 2 * HD)], b.kv_in.at[1], b.kv_s, b.kv_r, dict(y=flip(y, 2)))
    b.q_in[me] = b.qout[me, :, :NB]
    b.kv_in[0] = b.qout[me, :, NB:]

    def project(acc, i, slot):
        drain(b.wt.at[slot], b.wsem.at[slot])

        @pl.loop(0, ROWS // TILE)
        def _(r):
            at = pl.ds(pl.multiple_of(r * TILE, TILE), TILE)
            new = jnp.dot(b.hn[ORDER[i], at, :], b.wt[slot].reshape(KB, KB), preferred_element_type=F32)
            acc[at, :] = new + acc[at, :] if i else new

    fetch = lambda f, i, slot: f.load(ORDER[i], b.wt.at[slot], b.wsem.at[slot])
    fetch(fg, 0, 0)
    fu.z_send(1)
    fetch(fg, 1, 1)
    project(b.gacc, 0, 0)
    fu.z_send(2)
    fetch(fg, 2, 0)
    project(b.gacc, 1, 1)
    fo.z_first()
    fo.z_second()
    fg.last(1)
    fg.last(2)
    project(b.gacc, 2, 0)
    fetch(fg, 3, 1)
    fd.forward(0)
    fetch(fu, 0, 0)
    project(b.gacc, 3, 1)
    fd.z_send(1)
    fd.z_send(2)
    project(b.uacc, 0, 0)

    drain(b.kc, b.ld.at[1])
    drain(b.vc, b.ld.at[2])
    drain(b.q_in.at[first(NJ - 1)], b.q_r)
    drain(b.kv_in.at[1], b.kv_r)

    @pl.loop(0, MINE)
    def _(r):
        b.lenb[pl.ds(r, 1), :] = jnp.broadcast_to(lens[r], (1, HD)).astype(F32)
    i_half = lax.rem(lax.broadcasted_iota(jnp.int32, (MINE, HD), 1), HD // 2).astype(F32)
    angle = b.lenb[...] * jnp.power(ROPE_BASE, i_half * (-2.0 / HD))
    low = lax.broadcasted_iota(jnp.int32, (MINE, HD), 1) < HD // 2
    cos = jnp.cos(angle)
    sin = jnp.where(low, -jnp.sin(angle), jnp.sin(angle))
    rope = lambda v: v * cos + pltpu.roll(v, HD // 2, 1) * sin
    kv = (b.kv_in[0].astype(F32) + b.kv_in[1].astype(F32)).astype(BF16).astype(F32)
    b.kn[:, :HD] = rope(kv[:, :HD])
    b.kn[:, HD:] = kv[:, HD:]
    for xs in RING:
        for yh in range(NC):
            q = (b.q_in[yh * 4 + xs].astype(F32) + b.q_in[(yh + 2) * 4 + xs].astype(F32)).astype(BF16).astype(F32)
            for h in range(5):
                b.q3[pl.ds(xs * 10 + yh * 5 + h, MINE, stride=HEADS), :] = rope(q[:, h * HD:(h + 1) * HD])
    t_row = lax.broadcasted_iota(jnp.int32, (SEQ, HD), 0)
    t_col = lax.broadcasted_iota(jnp.int32, (HEADS, SEQ), 1)

    @pl.loop(0, MINE // 4)
    def _(step):
        for k in RING:
            r = step * 4 + k
            here = t_row == lens[r]
            new = b.kn[pl.ds(r, 1), :]
            keys = jnp.where(here, new[:, :HD].astype(BF16).astype(F32), b.kc[r].astype(F32)).astype(BF16)
            vals = jnp.where(here, new[:, HD:], b.vc[r].astype(F32)).astype(BF16)
            b.kc[r] = keys
            b.vc[r] = vals
            at = pl.ds(pl.multiple_of(r * HEADS, 8), HEADS)
            s = lax.dot_general(b.q3[at, :].astype(BF16), keys, NT, preferred_element_type=F32) * (HD ** -0.5)
            s = jnp.where(t_col <= lens[r], s, -1e30)
            e = jnp.exp(s - jnp.max(s, axis=1, keepdims=True))
            p = (e / jnp.sum(e, axis=1, keepdims=True)).astype(BF16)
            b.q3[at, :] = jnp.dot(p, vals, preferred_element_type=F32)
    get(b.kc, kc_o, b.out_l)
    get(b.vc, vc_o, b.out_l)
    for h in range(HEADS):
        b.o_v[:, h * HD:(h + 1) * HD] = b.q3[pl.ds(h, MINE, stride=HEADS), :].astype(BF16)
    block = lambda yy, xx: b.o_v.at[:, pl.ds(pl.multiple_of((xx * 2 + lax.rem(yy, 2)) * NB, LANE), NB)]
    for dy, dx in PAIRS:
        yy, xx = flip(y, dy), flip(x, dx)
        put(block(yy, xx), b.o_in.at[me], b.o_s, b.o_r, dict(y=yy, x=xx))
    b.o_in[me] = block(y, x)[...]

    fu.forward(1)
    fu.forward(2)
    fo.forward()
    fetch(fu, 1, 1)
    fetch(fu, 2, 0)
    project(b.uacc, 1, 1)
    fu.last(1)
    fu.last(2)
    project(b.uacc, 2, 0)
    fetch(fu, 3, 1)
    fetch(fd, 0, 0)
    load_o = lambda i: fo.load(ORDER[i], b.wo_t.at[i % 2], b.osem.at[i % 2])
    load_o(0)
    project(b.uacc, 3, 1)

    @pl.loop(0, ROWS // LANE)
    def _(r):
        at = pl.ds(pl.multiple_of(r * LANE, LANE), LANE)
        g = b.gacc[at, :].astype(BF16).astype(F32)
        b.act[at, :] = (g / (1.0 + jnp.exp(-g)) * b.uacc[at, :].astype(BF16).astype(F32)).astype(BF16)
    fd.forward(1)
    fd.forward(2)
    fo.last()

    drain(b.o_in.at[first(NJ - 1)], b.o_r)
    HA, HBk = first(CUT), pl.ds(CUT, ROWS - CUT)

    def multiply(i):
        dz, slot = ORDER[i], i % 2
        drain(b.wt.at[slot], b.wsem.at[slot])
        drain(b.wo_t.at[slot], b.osem.at[slot])
        if i > 1:
            old = ORDER[i - 2]
            drain(b.a1.at[old], b.a1s.at[old])
            drain(b.b1.at[old], b.b1s.at[old])

        def some(lo, hi):
            @pl.loop(lo // TILE, hi // TILE)
            def _(r):
                at = pl.ds(pl.multiple_of(r * TILE, TILE), TILE)
                out = lax.dot_general(b.wt[slot].reshape(KB, KB), b.act[at, :], NT, preferred_element_type=F32)
                rows = b.o_in[pl.ds(r * 4, 4)].reshape(TILE, NB)
                att = lax.dot_general(b.wo_t[slot].reshape(NB, NB), rows, NT, preferred_element_type=F32)
                b.sb[slot, first(2), :, at] = (out[:NB] + att).astype(BF16).reshape(2, HB, TILE)
                b.sb[slot, pl.ds(2, 2), :, at] = out[NB:].astype(BF16).reshape(2, HB, TILE)

        some(0, CUT)
        for d in AWAY:
            put(b.sb.at[slot, d, :, HA], b.a1.at[dz, d - 1], b.a1s.at[dz], b.a1r.at[dz], dict(y=flip(y, d)))
        some(CUT, ROWS)
        for d in AWAY:
            put(b.sb.at[slot, :, mine(d), HBk], b.b1.at[dz, d - 1], b.b1s.at[dz], b.b1r.at[dz], dict(x=flip(x, d)))

    def second(i):
        dz, slot = ORDER[i], i % 2
        drain(b.a1.at[dz], b.a1r.at[dz])
        get(b.a1.at[dz], b.va, b.vsem.at[0])
        drain(b.b1.at[dz], b.b1r.at[dz])
        get(b.b1.at[dz], b.vb, b.vsem.at[1])
        drain(b.va, b.vsem.at[0])
        b.s2a[dz] = (b.sb[slot, 0, :, HA].astype(F32) + three(b.va)).astype(BF16)
        for d in AWAY:
            put(b.s2a.at[dz, mine(d)], b.a2.at[dz, d - 1], b.a2s.at[dz], b.a2r.at[dz], dict(x=flip(x, d)))
        drain(b.vb, b.vsem.at[1])
        b.s2b[dz] = (b.sb[slot, :, mine(0), HBk].astype(F32) + three(b.vb)).astype(BF16)
        for d in AWAY:
            put(b.s2b.at[dz, d], b.b2.at[dz, d - 1], b.b2s.at[dz], b.b2r.at[dz], dict(y=flip(y, d)))

    def third(i):
        dz = ORDER[i]
        drain(b.a2.at[dz], b.a2r.at[dz])
        drain(b.b2.at[dz], b.b2r.at[dz])
        for src, own, lanes in ((b.a2, b.s2a[dz, mine(0)], HA), (b.b2, b.s2b[dz, 0], HBk)):
            total = own.astype(F32) + three(src.at[dz])
            for cc in range(NC):
                b.fs[dz, cc, :, lanes] = (b.F[dz * 2 + cc, :, lanes].astype(F32) + total[cc * FEATS:(cc + 1) * FEATS]).astype(BF16)
        at = z * 2 + c
        for cc in (c, 1 - c)[dz == 0:]:
            put(b.fs.at[dz, cc], b.fin.at[at], b.fin_s, b.fin_r.at[at], dict(z=flip(z, dz), c=cc))
        if dz == 0:
            b.fin[at] = b.fs[0, c]

    multiply(0)
    fetch(fd, 1, 1)
    load_o(1)
    fetch(fd, 2, 0)
    load_o(2)
    multiply(1)
    second(0)
    for g in range(3):
        fd.last(g)
    multiply(2)
    fetch(fd, 3, 1)
    load_o(3)
    second(1)
    third(0)
    multiply(3)
    second(2)
    third(1)
    second(3)
    third(2)
    third(3)

    for dz in AWAY + (0,):
        zz = flip(z, dz)
        for cc in (c, 1 - c)[dz == 0:]:
            drain(b.fin.at[zz * 2 + cc], b.fin_r.at[zz * 2 + cc])
        for p in range(NG):
            at = pl.ds(p * LANE, LANE)
            lo, hi = b.fin[zz * 2, :, at].astype(F32), b.fin[zz * 2 + 1, :, at].astype(F32)
            pair = [jnp.where(row_low, lo, pltpu.roll(hi, LANE // 2, 1)), jnp.where(row_low, pltpu.roll(lo, LANE // 2, 1), hi)]
            b.ov[:, pl.ds(pl.multiple_of(zz * 2 * ROWS + p * 2 * LANE, LANE), 2 * LANE)] = jnp.concatenate(pair, axis=1).astype(BF16)
    get(b.ov, outT, b.ld.at[0])

    drain(part_a(3), b.ag_s.at[0])
    drain(part_b(3), b.ag_s.at[1])
    drain(all_a, b.ag_s.at[2])
    drain(all_b, b.ag_s.at[3])
    drain(b.S.at[first(NJ - 1)], b.s_s)
    drain(b.F.at[first(7)], b.f_s)
    drain(b.q_in.at[first(NJ - 1)], b.q_s)
    drain(b.kv_in.at[1], b.kv_s)
    drain(b.o_in.at[first(NJ - 1)], b.o_s)
    for dz in ORDER:
        if dz in ORDER[2:]:
            drain(b.a1.at[dz], b.a1s.at[dz])
            drain(b.b1.at[dz], b.b1s.at[dz])
        drain(b.a2.at[dz], b.a2s.at[dz])
        drain(b.b2.at[dz], b.b2s.at[dz])
    drain(b.fin.at[first(7)], b.fin_s)
    for f in (fq, fg, fu, fd, fo):
        f.finish()
    for ref in (b.kc, b.vc):
        drain(ref, b.out_l)
    drain(b.ov, b.ld.at[0])


def solution(mesh):
    inner = Mesh(mesh.devices.reshape(4, 4, 4, 2), tuple('zyxc'))

    def layer(residual, ln_scale, w_query, w_key, w_value, w_gate, w_up, w_out, w_down, k_cache, v_cache, lengths):
        hbm = pl.BlockSpec(memory_space=pltpu.HBM)
        vmem = pl.BlockSpec(memory_space=pltpu.VMEM)
        smem = pl.BlockSpec(memory_space=pltpu.SMEM)
        shape = lambda a: jax.ShapeDtypeStruct(*a)
        outs = [((FEATS, BATCH), BF16), (k_cache.shape, BF16), (v_cache.shape, BF16)] + list(HBM_BUFS.values())
        res = pl.pallas_call(
            kernel,
            out_shape=[shape(a) for a in outs],
            in_specs=[hbm, vmem, smem] + [hbm] * 9,
            out_specs=[hbm] * len(outs),
            scratch_shapes=[pltpu.VMEM(*a) for a in VMEM_BUFS.values()] + [DMA(s) if s else DMA for s in SEMS.values()] + NARROW_SEMS + WIDE_SEMS * 3 + NARROW_SEMS,
            name='decode_layer',
            compiler_params=pltpu.CompilerParams(collective_id=0, has_side_effects=True, vmem_limit_bytes=67043328),
        )(residual.T, ln_scale.reshape(1, FEATS), lengths, w_query, w_key, w_value, w_gate, w_up, w_down.T, w_out.T, k_cache, v_cache)
        return res[0].T, res[1], res[2]

    rc, tx, tyz = tuple('zyxc'), tuple('zy'), tuple('xc')
    cache = P(rc, None, None)
    in_specs = (P(None, rc), P(rc), P(tx, tyz), P(tx, None), P(tx, None), P(tx, tyz), P(tx, tyz), P(tyz, tx), P(tyz, tx), cache, cache, P(rc))
    return jax.shard_map(layer, mesh=inner, in_specs=in_specs, out_specs=(P(None, rc), cache, cache), check_vma=False)
```

time: 1330 us -> 322 us (0.24)
  waiting for transfers between devices: 1120 us -> 0 us
  Pallas kernels: 0 us -> 315 us
  matrix products: 125 us -> 0 us
  other arithmetic: 20.3 us -> 0 us
  local copies, waits for them, and re-layouts: 22.5 us -> 5.29 us
  blocking collectives: 14.4 us -> 0 us
  between operations: 14.3 us -> 0.65 us
    reduce_scatter x6 -> x0, waiting for transfers between devices: 632 us -> none  [the longest x1 240 us: decode_layer(): lax.psum_scatter(gate_part, 'tx', scatter_dimension=1, tiled=True)]
    all_gather x3 -> x0, waiting for transfers between devices: 329 us -> none  [the longest x1 217 us: decode_layer(): act_full = lax.all_gather(mlp_act, 'tx', axis=1, tiled=True)]
    pallas_call x0 -> x1, Pallas kernels: none -> 315 us  [layer(): pl.pallas_call(kernel, out_shape=[shape(a) for a in outs], in_specs=[hbm,...]
    psum x1 -> x0, waiting for transfers between devices: 152 us -> none  [decode_layer(): row_stats = lax.psum(row_stats, ('tx', 'tyz'))]
    dot_general x9 -> x0, matrix products: 124 us -> none  [the longest x1 29.1 us: decode_layer(): jnp.dot(normed_tx, w_gate, preferred_element_type=jnp.float32)]
    all_to_all x1 -> x0, blocking collectives: 14.4 us -> none  [decode_layer(): attended_heads = lax.all_to_all(attended, 'tyz', 1, 0, tiled=True)]
    all_gather x1 -> x0, local copies, waits for them, and re-layouts: 14.2 us -> none  [decode_layer(): attended_all = lax.all_gather(attended_heads, 'tx', axis=0, tiled=True)]
  transfers between devices with their start and end apart: 11 -> 0, of which waited for: 10 -> 0; matrix products, arithmetic and copies ran while one was open for 10% -> 0% of each run, Pallas kernels for 0% -> 0%
where the time goes in v2:
time: 322 us; the launch traced here: 321 us
  Pallas kernels  315 us (98%)
  local copies, waits for them, and re-layouts  5.29 us (2%)
    pallas_call x1, Pallas kernels, layer(): pl.pallas_call(kernel, out_shape=[shape(a) for a in outs], in_specs=[hbm,...  315 us

profile of v2, /device:TPU:1, one launch (start us, length us, event | category | flops | bytes accessed | tf_op | source)
XLA Modules:
  0.0 321.3 jit_solution(439429602630587835)
XLA Ops:
  0.6 315.3 %decode_layer.1 = (bf16[40,8192]{1,0:T(8,128)(2,1)}, bf16[64,64,128]{2,1,0:T(8,128)(2,1)}, bf16[64,64,128]{2,1,0:T(8,128)(2,1)}, bf16[8,320,896]{2,1,0:T(8,128)(...) custom-call(bf16[40,8192]{1,0:T(8,128)(2,1)} %bitcast.6, ...), custom_call_target="tpu_custom_call" | custom-call | tf_op jit(solution)/shard_map/decode_layer/pallas_call | solution.py:593
  316.0 0.0 copy-start
  316.0 2.1 copy.18
  318.0 2.3 copy.19
  320.3 0.0 copy-done
  320.3 1.0 copy.20
Async XLA Ops:
  316.0 4.3 %copy-start = (bf16[64,64,128]{2,1,0:T(8,128)(2,1)S(1)}, bf16[64,64,128]{2,1,0:T(8,128)(2,1)}, u32[]{:S(2)}) copy-start(bf16[64,64,128]{2,1,0:T(8,128)(2,1)} %get-tuple-element.14) | copy-start | bytes 3145732

commit v3 on v2

v3 whole, which is shorter than its diff:
```python
import jax
import jax.numpy as jnp
from jax import lax
from jax.experimental import pallas as pl
from jax.experimental.pallas import tpu as pltpu
from jax.sharding import Mesh, PartitionSpec as P

LN_EPS = 1e-5
ROPE_BASE = 10000.0
MESH = pl.DeviceIdType.MESH
DMA = pltpu.SemaphoreType.DMA
F32, BF16 = jnp.float32, jnp.bfloat16
ROWS, MODEL, FEATS, BATCH = 1024, 5120, 40, 8192
KB, NB, HB, QB, HD, SUB = 1280, 640, 320, 896, 128, 80
MINE, SEQ, HEADS, LANE, HALF = 64, 64, 40, 128, 64
NR, NC, NJ, NG = 4, 2, 16, 8
X_FIRST = (1,)
CUT = 512
TILE = 256
RING = range(4)
AWAY = (1, 3, 2)
SIDES = AWAY[:2]
FORTH, BACK = ((1, 0), (3, 1)), ((3, 0), (1, 1))
GROUPS = ((0, 1), (1, 2), (2, 4))
ORDER = (0, 1, 3, 2)
PAIRS = tuple(sorted(((dy, dx) for dy in RING for dx in RING if dy or dx), key=lambda p: (p.count(2), 0 not in p, abs(p[0] - p[1]))))
NT = (((1,), (1,)), ((), ()))


def flip(i, d):
    return (i, i + 1 - 2 * lax.rem(i, 2), lax.rem(i + 2, 4), 3 - i)[d]


def put(src, dst, ssem, rsem, dev):
    pltpu.make_async_remote_copy(src_ref=src, dst_ref=dst, send_sem=ssem, recv_sem=rsem, device_id=dev, device_id_type=MESH).start()


def added(ref):
    return sum(ref[k].astype(F32) for k in range(NR - 1))


def get(src, dst, sem):
    pltpu.make_async_copy(src, dst, sem).start()


def first(n):
    return pl.ds(0, n)


def drain(ref, sem):
    pltpu.make_async_copy(ref, ref, sem).wait()


class Wide:
    def __init__(self, land, src, sems, pos):
        self.land, self.src = land, src
        self.send, self.yr, self.zr, self.fr, self.dr, self.loc = sems
        self.z, self.y, self.x, self.c = pos
        self.base = self.c * 16
        self.here = set()

    def piece(self, yy):
        return self.src.at[:, pl.ds(pl.multiple_of(yy * NB, LANE), NB)]

    def at(self, dz, g, base=None):
        lo, hi = GROUPS[g]
        return self.land.at[pl.ds((self.base if base is None else base) + dz * 4 + lo, hi - lo)]

    def start_local(self):
        get(self.piece(self.y), self.land.at[self.base], self.loc)

    def y_send(self):
        for dy in AWAY:
            yy = flip(self.y, dy)
            put(self.piece(yy), self.land.at[self.base + dy], self.send, self.yr.at[dy - 1], dict(y=yy))

    def z_send(self, g):
        if g:
            for dy in range(*GROUPS[g]):
                drain(self.land.at[self.base + dy], self.yr.at[dy - 1])
        for k, dz in enumerate(SIDES):
            to = dict(z=flip(self.z, dz))
            if g:
                put(self.at(0, g), self.at(dz, g), self.send, self.zr.at[k * 3 + g], to)
            else:
                put(self.piece(self.y), self.land.at[self.base + dz * 4], self.send, self.zr.at[k * 3], to)
        self.d2d(0, g)

    def forward(self, g):
        for k, dz in enumerate(SIDES):
            drain(self.at(dz, g), self.zr.at[k * 3 + g])
        for k, dz in enumerate(SIDES):
            put(self.half(dz, g, k), self.half(2, g, k), self.send, self.fr.at[g], dict(z=flip(self.z, AWAY[1 - k])))
            self.d2d(dz, g)

    def half(self, dz, g, k):
        lo, hi = GROUPS[g]
        return self.land.at[pl.ds(self.base + dz * 4 + lo, hi - lo), pl.ds(k * HB // 2, HB // 2)]

    def last(self, g):
        drain(self.at(2, g), self.fr.at[g])
        self.d2d(2, g)

    def d2d(self, dz, g):
        to = dict(c=1 - self.c)
        if dz or g:
            put(self.at(dz, g), self.at(dz, g), self.send, self.dr.at[dz * 3 + g], to)
        else:
            put(self.piece(self.y), self.land.at[self.base], self.send, self.dr.at[0], to)

    def load(self, dz, tile, sem):
        if dz not in self.here:
            if dz == 0:
                drain(self.land.at[self.base], self.loc)
            for g in range(len(GROUPS)):
                drain(self.at(dz, g, 16 - self.base), self.dr.at[dz * 3 + g])
        self.here.add(dz)
        for cc in range(NC):
            get(self.land.at[pl.ds(cc * 16 + dz * 4, 4)], tile.at[:, :, pl.ds(cc * NB, NB)], sem)

    def finish(self):
        drain(self.land.at[first(31)], self.send)


class Narrow:
    def __init__(self, land, parts, sems, pos):
        self.land, self.parts = land, parts
        self.send, self.yr, self.zr, self.fr, self.dr, self.loc = sems
        self.z, self.y, self.x, self.c = pos
        self.s = lax.rem(self.c + self.y, 2)

    def own(self, slot):
        lo = 0
        for ref in self.parts:
            hi = lo + ref.shape[1]
            yield ref, self.land.at[slot, :, pl.ds(lo, hi - lo)]
            lo = hi

    def start(self):
        @pl.when(self.s == 0)
        def _():
            for src, dst in self.own(0):
                get(src, dst, self.loc)

        @pl.when(self.s == 1)
        def _():
            for src, dst in self.own(1):
                put(src, dst, self.send, self.yr, dict(y=flip(self.y, 1), c=1 - self.c))

    def z_first(self):
        @pl.when(self.s == 0)
        def _():
            for k, dz in enumerate(SIDES):
                for (src, _), (_, dst) in zip(self.own(0), self.own(dz * 2)):
                    put(src, dst, self.send, self.zr.at[k], dict(z=flip(self.z, dz)))
            for src, dst in self.own(0):
                put(src, dst, self.send, self.dr.at[0], dict(c=1 - self.c))

    def z_second(self):
        @pl.when(self.s == 1)
        def _():
            src = self.land.at[1]
            drain(src, self.yr)
            for k, dz in enumerate(SIDES):
                put(src, self.land.at[dz * 2 + 1], self.send, self.zr.at[k], dict(z=flip(self.z, dz)))
            put(src, src, self.send, self.dr.at[0], dict(c=1 - self.c))

    def half(self, slot, k):
        return self.land.at[slot, pl.ds(k * HB // 2, HB // 2)]

    def forward(self):
        for k, dz in enumerate(SIDES):
            slot = dz * 2 + self.s
            piece = self.land.at[slot]
            drain(piece, self.zr.at[k])
            put(self.half(slot, k), self.half(4 + self.s, k), self.send, self.fr.at[k], dict(z=flip(self.z, AWAY[1 - k])))
            put(piece, piece, self.send, self.dr.at[1 + k], dict(c=1 - self.c))

    def last(self):
        for k in range(NC):
            piece = self.half(4 + self.s, k)
            drain(piece, self.fr.at[k])
            put(piece, piece, self.send, self.dr.at[3 + k], dict(c=1 - self.c))

    def load(self, dz, tile, sem):
        o = 1 - self.s
        if dz == 0:
            @pl.when(self.s == 0)
            def _():
                drain(self.land.at[0], self.loc)
        if dz == 2:
            for k in range(NC):
                drain(self.half(4 + o, k), self.dr.at[3 + k])
        else:
            drain(self.land.at[dz * 2 + o], self.dr.at[(dz + 1) // 2])
        get(self.land.at[pl.ds(dz * 2, 2)], tile, sem)

    def finish(self):
        for s in range(NC):
            @pl.when(self.s == s)
            def _():
                drain(self.land.at[first(7 + s)], self.send)


class Ring:
    def __init__(self, axis, at, own, land, moved, sems):
        self.axis, self.at, self.own, self.land, self.moved = axis, at, own, land, moved
        self.send, self.recv = sems

    def to(self, d):
        return {self.axis: flip(self.at, d)}

    def start(self):
        for k in range(NC):
            for d, h in ((1, k), (3, 1 - k)):
                put(self.own(h), self.land(d, h), self.send, self.recv.at[d - 1 + h], self.to(d))

    def forward(self):
        for d, h in FORTH:
            drain(self.moved(d, h), self.recv.at[d - 1 + h])
            put(self.moved(d, h), self.moved(2, h) if self.axis == 'y' else self.moved(d, h), self.send, self.recv.at[4 + h], self.to(4 - d))

    def finish(self):
        for d, h in BACK:
            drain(self.moved(d, h), self.recv.at[d - 1 + h])
        for h in range(NC):
            drain(self.moved(2, h), self.recv.at[4 + h])


WIDE_SEMS = [DMA, DMA((3,)), DMA((6,)), DMA((3,)), DMA((12,)), DMA]
NARROW_SEMS = [DMA, DMA, DMA((2,)), DMA((2,)), DMA((5,)), DMA]
HBM_BUFS = dict(
    Q=((NG, HB, QB), BF16), G=((NG * NR, HB, NB), BF16), U=((NG * NR, HB, NB), BF16), D=((NG * NR, HB, NB), BF16), O=((NG, HB, NB), BF16),
    hnT=((NR, NR, HB, ROWS), BF16), a1=((NR, NC, HB, CUT), BF16), b1=((NR, NC, NR, SUB, ROWS - CUT), BF16))
VMEM_BUFS = dict(
    rT=((FEATS, BATCH), BF16), xs=((NG, FEATS, ROWS + LANE), BF16), F=((NG, FEATS, ROWS + LANE), BF16), S=((NC, NJ, 2, CUT), F32),
    hs=((NR, SUB, ROWS), BF16), hn=((NR, ROWS, KB), BF16), wt=((NC, NR, HB, KB), BF16), wo_t=((NC, NC, HB, NB), BF16),
    gacc=((ROWS, KB), F32), uacc=((ROWS, KB), F32), qout=((NJ, MINE, QB), BF16), q_in=((NJ, MINE, NB), BF16), kv_in=((NC, MINE, 2 * HD), BF16),
    q3=((MINE * HEADS, HD), F32), lenb=((MINE, HD), F32), kc=((MINE, SEQ, HD), BF16), vc=((MINE, SEQ, HD), BF16), kn=((MINE, 2 * HD), F32),
    o_v=((MINE, MODEL), BF16), o_in=((NJ, MINE, NB), BF16), act=((ROWS, KB), BF16), sb=((NR - 1, NR, HB, ROWS), BF16),
    va=((NC, HB, CUT), BF16), vb=((NC, NR, SUB, ROWS - CUT), BF16),
    ta=((NR, NC, HB // 2, CUT), BF16), tb=((NR, NC, NR // 2, SUB, ROWS - CUT), BF16), s2a=((NR, HB, CUT), BF16), s2b=((NR, NR, SUB, ROWS - CUT), BF16),
    a2=((NR, NR - 1, SUB, CUT), BF16), b2=((NR, NR - 1, SUB, ROWS - CUT), BF16), fs=((NR, NC, FEATS, ROWS), BF16))
ONE, EACH, BY_GROUP = (), (NR,), (NG,)
SEMS = dict(f_s=ONE, fin_l=ONE, s_s=EACH, s_r=EACH, own_l=EACH, q_s=ONE, q_r=ONE, kv_s=ONE, kv_r=ONE, o_s=ONE, o_r=ONE, fin_s=ONE, out_l=ONE,
            a1s=EACH, a1r=EACH, b1s=EACH, b1r=EACH, a2s=EACH, a2r=EACH, b2s=EACH, b2r=EACH, ag_s=BY_GROUP, ag_r=(NG, NG), tas=EACH, tbs=EACH, tar=BY_GROUP, tbr=BY_GROUP, ld=EACH, wsem=EACH, osem=EACH, vsem=EACH,
            f_r=(NC, NG), fin_r=BY_GROUP)


def kernel(res, ls, lens, wq, wk, wv, wg, wu, wdT, woT, kc_h, vc_h, fin, kc_o, vc_o, *rest):
    rest = list(rest)

    class b:
        pass
    for name in list(HBM_BUFS) + list(VMEM_BUFS) + list(SEMS):
        setattr(b, name, rest.pop(0))
    pos = z, y, x, c = tuple(lax.axis_index(a) for a in 'zyxc')
    flow = lambda kind, land, src: kind(land, src, [rest.pop(0) for _ in WIDE_SEMS], pos)
    fq = flow(Narrow, b.Q, (wq, wk, wv))
    fg, fu, fd = flow(Wide, b.G, wg), flow(Wide, b.U, wu), flow(Wide, b.D, wdT)
    fo = flow(Narrow, b.O, (woT,))
    me = y * 4 + x
    row_low = lax.broadcasted_iota(jnp.int32, (FEATS, LANE), 1) < HALF
    sides = lambda dz: (c, 1 - c)[not dz:]

    bar = pltpu.get_barrier_semaphore()
    peers = [dict(z=flip(z, dz), c=cc) for dz in AWAY for cc in (c, 1 - c)] + [dict(c=1 - c), dict(y=flip(y, 1), c=1 - c)]
    peers += [dict(y=flip(y, dy), x=flip(x, dx)) for dy, dx in PAIRS]
    for p in peers:
        pl.semaphore_signal(bar, inc=1, device_id=p, device_id_type=MESH)
    get(res, b.rT, b.ld.at[0])
    get(kc_h, b.kc, b.ld.at[1])
    get(vc_h, b.vc, b.ld.at[2])
    for f in (fg, fu, fd):
        f.start_local()
    pl.semaphore_wait(bar, len(peers))
    fq.start()

    drain(b.rT, b.ld.at[0])
    scale = jnp.broadcast_to(ls[...].astype(F32), (LANE, FEATS)).T.astype(BF16)
    wide = lambda h: pl.ds(LANE * h + CUT * h, CUT + LANE * (1 - h))
    for i in range(NG):
        b.xs[i, :, :LANE] = scale
    for h in range(NC):
        for dz in AWAY + (0,):
            zz = flip(z, dz)
            for p in range(NR * h, NR * h + NR):
                pair = b.rT[:, pl.ds(pl.multiple_of(zz * NC * ROWS + p * TILE, LANE), TILE)].astype(F32)
                t0, t1 = pair[:, :LANE], pair[:, LANE:]
                at = pl.ds(LANE + p * LANE, LANE)
                b.xs[dz * NC, :, at] = jnp.where(row_low, t0, pltpu.roll(t1, HALF, 1)).astype(BF16)
                b.xs[dz * NC + 1, :, at] = jnp.where(row_low, pltpu.roll(t0, HALF, 1), t1).astype(BF16)
            for cc in sides(dz):
                put(b.xs.at[dz * NC + cc, :, wide(h)], b.F.at[dz * NC + c, :, wide(h)], b.f_s, b.f_r.at[h, dz * NC + c], dict(z=flip(z, dz), c=cc))
    b.F[c] = b.xs[c]
    fq.z_first()
    fg.z_send(0)

    for h in range(NC):
        for dz in RING:
            for cc in sides(dz):
                drain(b.F.at[dz * NC + cc, :, wide(h)], b.f_r.at[h, dz * NC + cc])
        tot = sq = jnp.zeros((FEATS, CUT), F32)
        for i in range(NG):
            v = b.F[i, :, pl.ds(LANE + CUT * h, CUT)].astype(F32)
            tot, sq = tot + v, sq + v * v
        b.S[h, me] = jnp.concatenate([jnp.sum(v, axis=0, keepdims=True) for v in (tot, sq)], axis=0)
        for dy, dx in PAIRS:
            put(b.S.at[h, me], b.S.at[h, me], b.s_s.at[h], b.s_r.at[h], dict(y=flip(y, dy), x=flip(x, dx)))
    fq.z_second()

    mine = lambda d: pl.ds(pl.multiple_of(flip(x, d) * SUB, 16), SUB)

    def normalize(h):
        drain(b.S.at[h, first(NJ - 1)], b.s_r.at[h])
        stats = sum(b.S[h, i] for i in range(NJ)) / MODEL
        mean = stats[0:1]
        inv = lax.rsqrt(stats[1:] - mean * mean + LN_EPS)
        lanes = pl.ds(CUT * h, CUT)
        for dz in RING:
            both = []
            for i in (dz * NC, dz * NC + 1):
                both.append((b.F[i, :, pl.ds(LANE + CUT * h, CUT)].astype(F32) - mean) * inv * b.F[i, :, :LANE].astype(F32)[:, :1])
            b.hs[dz, :, lanes] = jnp.concatenate(both, axis=0).astype(BF16)
        get(b.hs.at[:, :, lanes], b.hnT.at[:, 0, mine(0), lanes], b.own_l.at[h])

    part = lambda h: pl.ds(2 * h, 2)

    def rings(k):
        lanes = pl.ds(k * TILE, TILE)
        far = lambda d, h: b.hnT.at[part(h), :, mine(d), lanes]
        near = lambda d, h: b.hnT.at[part(h), d, mine(0), lanes]
        own = lambda h: b.hs.at[part(h), :, lanes]
        sems = [(b.ag_s.at[NC * k + j], b.ag_r.at[NC * k + j]) for j in range(NC)]
        if k in X_FIRST:
            spot = lambda d, h: b.hnT.at[part(h), 0, mine(d), lanes]
            row = lambda d, h: b.hnT.at[part(h), d, :, lanes]
            return Ring('x', x, own, lambda d, h: spot(0, h), spot, sems[0]), Ring('y', y, lambda h: row(0, h), row, row, sems[1])
        return Ring('y', y, own, near, near, sems[0]), Ring('x', x, lambda h: far(0, h), lambda d, h: far(0, h), far, sems[1])

    one, two = zip(*(rings(k) for k in RING))
    normalize(0)
    one[0].start()
    one[1].start()
    one[0].forward()
    one[1].forward()
    normalize(1)
    one[2].start()
    one[3].start()
    for h in range(NC):
        drain(b.hs.at[:, :, pl.ds(CUT * h, CUT)], b.own_l.at[h])
    one[0].finish()
    two[0].start()
    one[2].forward()
    one[3].forward()
    fg.y_send()
    one[1].finish()
    two[1].start()
    two[0].forward()
    fq.forward()
    fg.forward(0)
    one[2].finish()
    two[2].start()
    one[3].finish()
    fg.z_send(1)
    fq.last()

    def load_q(pair):
        for i in range(NC):
            fq.load(NC * pair + i, b.sb.at[pair, part(i), :, first(QB)], b.osem.at[pair])

    def stage(k):
        two[k].finish()
        for dz in RING:
            get(b.hnT.at[dz, :, :, pl.ds(k * TILE, TILE)], b.wt.at[1, :, :, pl.ds(dz * TILE, TILE)], b.wsem.at[1])

    def turn(k):
        drain(b.wt.at[1, :, :, first(ROWS)], b.wsem.at[1])
        for dz in RING:
            for h in range(NC):
                b.hn[dz, pl.ds(k * TILE + h * LANE, LANE), :] = b.wt[1, :, :, pl.ds(dz * TILE + h * LANE, LANE)].reshape(KB, LANE).T

    def query(k):
        at = pl.ds(k * TILE, TILE)
        new = sum(jnp.dot(b.hn[dz, at, :NB], b.sb[dz // 2, part(dz % 2), :, :QB].reshape(NB, QB), preferred_element_type=F32) for dz in RING)
        b.qout[pl.ds(k * NR, NR)] = new.astype(BF16).reshape(NR, MINE, QB)

    def project(acc, i, slot, lo=0, hi=ROWS, fresh=False, wait=True):
        if wait:
            drain(b.wt.at[slot], b.wsem.at[slot])

        @pl.loop(lo // TILE, hi // TILE)
        def _(r):
            at = pl.ds(pl.multiple_of(r * TILE, TILE), TILE)
            new = jnp.dot(b.hn[ORDER[i], at, :], b.wt[slot].reshape(KB, KB), preferred_element_type=F32)
            acc[at, :] = new if fresh else new + acc[at, :]

    fetch = lambda f, i, slot: f.load(ORDER[i], b.wt.at[slot], b.wsem.at[slot])
    fg.z_send(2)
    fu.z_send(0)
    load_q(0)
    load_q(1)
    stage(0)
    two[2].forward()
    two[3].start()
    turn(0)
    for pair in range(NC):
        drain(b.sb.at[pair, :, :, first(QB)], b.osem.at[pair])
    query(0)
    two[1].forward()
    fu.y_send()
    fg.forward(1)
    stage(2)
    turn(2)
    query(2)
    fetch(fg, 0, 0)
    two[3].forward()
    stage(1)
    turn(1)
    query(1)
    fg.forward(2)
    fg.last(0)
    project(b.gacc, 0, 0, 0, 3 * TILE, fresh=True)
    fu.z_send(1)
    fu.forward(0)
    fetch(fg, 1, 0)
    project(b.gacc, 1, 0, 0, 3 * TILE)
    fu.z_send(2)
    stage(3)
    turn(3)
    fetch(fg, 0, 1)
    query(3)
    for dy, dx in PAIRS:
        yy, xx = flip(y, dy), flip(x, dx)
        put(b.qout.at[yy * NR + xx, :, first(NB)], b.q_in.at[me], b.q_s, b.q_r, dict(y=yy, x=xx))
    put(b.qout.at[flip(y, 2) * NR + x, :, pl.ds(NB, 2 * HD)], b.kv_in.at[1], b.kv_s, b.kv_r, dict(y=flip(y, 2)))
    b.q_in[me] = b.qout[me, :, :NB]
    b.kv_in[0] = b.qout[me, :, NB:]
    fo.start()
    fd.y_send()

    project(b.gacc, 1, 0, 3 * TILE, ROWS, fresh=True, wait=False)
    fetch(fg, 2, 0)
    project(b.gacc, 0, 1, 3 * TILE, ROWS)
    fg.last(1)
    fg.last(2)
    fetch(fg, 3, 1)
    project(b.gacc, 2, 0)
    fu.forward(1)
    fetch(fu, 0, 0)
    project(b.gacc, 3, 1)
    project(b.uacc, 0, 0, fresh=True)
    drain(b.kc, b.ld.at[1])
    drain(b.vc, b.ld.at[2])
    drain(b.q_in.at[first(NJ - 1)], b.q_r)
    drain(b.kv_in.at[1], b.kv_r)

    @pl.loop(0, MINE)
    def _(r):
        b.lenb[pl.ds(r, 1), :] = jnp.broadcast_to(lens[r], (1, HD)).astype(F32)
    i_half = lax.rem(lax.broadcasted_iota(jnp.int32, (MINE, HD), 1), HALF).astype(F32)
    angle = b.lenb[...] * jnp.power(ROPE_BASE, i_half * (-2.0 / HD))
    low = lax.broadcasted_iota(jnp.int32, (MINE, HD), 1) < HALF
    cos = jnp.cos(angle)
    sin = jnp.where(low, -jnp.sin(angle), jnp.sin(angle))
    rope = lambda v: v * cos + pltpu.roll(v, HALF, 1) * sin
    kv = (b.kv_in[0].astype(F32) + b.kv_in[1].astype(F32)).astype(BF16).astype(F32)
    b.kn[:, :HD] = rope(kv[:, :HD])
    b.kn[:, HD:] = kv[:, HD:]
    for xs in RING:
        for yh in range(NC):
            q = (b.q_in[yh * 4 + xs].astype(F32) + b.q_in[(yh + 2) * 4 + xs].astype(F32)).astype(BF16).astype(F32)
            for h in range(5):
                b.q3[pl.ds(xs * 10 + yh * 5 + h, MINE, stride=HEADS), :] = rope(q[:, h * HD:(h + 1) * HD])
    t_row = lax.broadcasted_iota(jnp.int32, (SEQ, HD), 0)
    t_col = lax.broadcasted_iota(jnp.int32, (HEADS, SEQ), 1)

    def attend(r):
        here = t_row == lens[r]
        new = b.kn[pl.ds(r, 1), :]
        keys = jnp.where(here, new[:, :HD].astype(BF16).astype(F32), b.kc[r].astype(F32)).astype(BF16)
        vals = jnp.where(here, new[:, HD:], b.vc[r].astype(F32)).astype(BF16)
        b.kc[r] = keys
        b.vc[r] = vals
        at = pl.ds(pl.multiple_of(r * HEADS, 8), HEADS)
        s = lax.dot_general(b.q3[at, :].astype(BF16), keys, NT, preferred_element_type=F32) * (HD ** -0.5)
        s = jnp.where(t_col <= lens[r], s, -1e30)
        e = jnp.exp(s - jnp.max(s, axis=1, keepdims=True))
        p = (e / jnp.sum(e, axis=1, keepdims=True)).astype(BF16)
        b.q3[at, :] = jnp.dot(p, vals, preferred_element_type=F32)

    def attend_some(lo, hi):
        @pl.loop(lo // NR, hi // NR)
        def _(step):
            for k in RING:
                attend(step * NR + k)

    attend_some(0, MINE // 4)
    fu.forward(2)
    fo.z_first()
    fo.z_second()
    fd.z_send(0)
    fd.z_send(1)
    attend_some(MINE // 4, MINE)
    get(b.kc, kc_o, b.out_l)
    get(b.vc, vc_o, b.out_l)
    for h in range(HEADS):
        b.o_v[:, h * HD:(h + 1) * HD] = b.q3[pl.ds(h, MINE, stride=HEADS), :].astype(BF16)
    block = lambda yy, xx: b.o_v.at[:, pl.ds(pl.multiple_of((xx * 2 + lax.rem(yy, 2)) * NB, LANE), NB)]
    for dy, dx in PAIRS:
        yy, xx = flip(y, dy), flip(x, dx)
        put(block(yy, xx), b.o_in.at[me], b.o_s, b.o_r, dict(y=yy, x=xx))
    b.o_in[me] = block(y, x)[...]

    fd.z_send(2)
    fetch(fu, 1, 1)
    fetch(fu, 2, 0)
    project(b.uacc, 1, 1)
    fu.last(0)
    fu.last(1)
    fu.last(2)
    project(b.uacc, 2, 0)
    fetch(fu, 3, 1)
    fetch(fd, 0, 0)
    load_o = lambda i: fo.load(ORDER[i], b.wo_t.at[i % 2], b.osem.at[i % 2])
    load_o(0)
    project(b.uacc, 3, 1)

    @pl.loop(0, ROWS // LANE)
    def _(r):
        at = pl.ds(pl.multiple_of(r * LANE, LANE), LANE)
        g = b.gacc[at, :].astype(BF16).astype(F32)
        b.act[at, :] = (g / (1.0 + jnp.exp(-g)) * b.uacc[at, :].astype(BF16).astype(F32)).astype(BF16)
    fo.forward()

    drain(b.o_in.at[first(NJ - 1)], b.o_r)
    HA, HBk = first(CUT), pl.ds(CUT, ROWS - CUT)

    def sent(dz):
        for land, sem in ((b.a1, b.a1s), (b.b1, b.b1s), (b.ta, b.tas), (b.tb, b.tbs)):
            drain(land.at[dz], sem.at[dz])

    def multiply(i):
        dz, slot = ORDER[i], i % 2
        drain(b.wt.at[slot], b.wsem.at[slot])
        drain(b.wo_t.at[slot], b.osem.at[slot])
        if i == 3:
            sent(ORDER[0])

        def some(lo, hi):
            @pl.loop(lo // TILE, hi // TILE)
            def _(r):
                at = pl.ds(pl.multiple_of(r * TILE, TILE), TILE)
                out = lax.dot_general(b.wt[slot].reshape(KB, KB), b.act[at, :], NT, preferred_element_type=F32)
                rows = b.o_in[pl.ds(r * 4, 4)].reshape(TILE, NB)
                att = lax.dot_general(b.wo_t[slot].reshape(NB, NB), rows, NT, preferred_element_type=F32)
                b.sb[i % 3, first(2), :, at] = (out[:NB] + att).astype(BF16).reshape(2, HB, TILE)
                b.sb[i % 3, pl.ds(2, 2), :, at] = out[NB:].astype(BF16).reshape(2, HB, TILE)

        some(0, CUT)
        half = HB // 2
        for d, h in FORTH:
            rows = pl.ds(h * half, half)
            put(b.sb.at[i % 3, 2, rows, HA], b.ta.at[dz, h], b.tas.at[dz], b.tar.at[2 * dz + h], dict(y=flip(y, d)))
            put(b.sb.at[i % 3, d, rows, HA], b.a1.at[dz, h, rows], b.a1s.at[dz], b.a1r.at[dz], dict(y=flip(y, d)))
        some(CUT, ROWS)
        for d, h in FORTH:
            dys = pl.ds(2 * h, 2)
            put(b.sb.at[i % 3, dys, mine(2), HBk], b.tb.at[dz, h], b.tbs.at[dz], b.tbr.at[2 * dz + h], dict(x=flip(x, d)))
            put(b.sb.at[i % 3, dys, mine(d), HBk], b.b1.at[dz, h, dys], b.b1s.at[dz], b.b1r.at[dz], dict(x=flip(x, d)))

    def passed(i):
        dz, slot = ORDER[i], i % 3
        half = HB // 2
        for d, h in BACK:
            rows = pl.ds(h * half, half)
            drain(b.ta.at[dz, h], b.tar.at[2 * dz + h])
            b.sb[slot, d, rows, HA] = (b.sb[slot, d, rows, HA].astype(F32) + b.ta[dz, h].astype(F32)).astype(BF16)
            put(b.sb.at[slot, d, rows, HA], b.a1.at[dz, 1 - h, rows], b.a1s.at[dz], b.a1r.at[dz], dict(y=flip(y, d)))
        for d, h in BACK:
            dys = pl.ds(2 * h, 2)
            drain(b.tb.at[dz, h], b.tbr.at[2 * dz + h])
            b.sb[slot, dys, mine(d), HBk] = (b.sb[slot, dys, mine(d), HBk].astype(F32) + b.tb[dz, h].astype(F32)).astype(BF16)
            put(b.sb.at[slot, dys, mine(d), HBk], b.b1.at[dz, 1 - h, dys], b.b1s.at[dz], b.b1r.at[dz], dict(x=flip(x, d)))

    def second(i):
        dz, slot = ORDER[i], i % 3
        drain(b.a1.at[dz], b.a1r.at[dz])
        get(b.a1.at[dz], b.va, b.vsem.at[0])
        drain(b.b1.at[dz], b.b1r.at[dz])
        get(b.b1.at[dz], b.vb, b.vsem.at[1])
        drain(b.va, b.vsem.at[0])
        b.s2a[dz] = (b.sb[slot, 0, :, HA].astype(F32) + (b.va[0].astype(F32) + b.va[1].astype(F32))).astype(BF16)
        for d in AWAY:
            put(b.s2a.at[dz, mine(d)], b.a2.at[dz, d - 1], b.a2s.at[dz], b.a2r.at[dz], dict(x=flip(x, d)))
        drain(b.vb, b.vsem.at[1])
        b.s2b[dz] = (b.sb[slot, :, mine(0), HBk].astype(F32) + (b.vb[0].astype(F32) + b.vb[1].astype(F32))).astype(BF16)
        for d in AWAY:
            put(b.s2b.at[dz, d], b.b2.at[dz, d - 1], b.b2s.at[dz], b.b2r.at[dz], dict(y=flip(y, d)))

    def third(i):
        dz = ORDER[i]
        drain(b.a2.at[dz], b.a2r.at[dz])
        drain(b.b2.at[dz], b.b2r.at[dz])
        for src, own, lanes, shifted in ((b.a2, b.s2a[dz, mine(0)], HA, pl.ds(LANE, CUT)), (b.b2, b.s2b[dz, 0], HBk, pl.ds(LANE + CUT, ROWS - CUT))):
            total = own.astype(F32) + added(src.at[dz])
            for cc in range(NC):
                b.fs[dz, cc, :, lanes] = (b.F[dz * 2 + cc, :, shifted].astype(F32) + total[cc * FEATS:(cc + 1) * FEATS]).astype(BF16)
        at = z * 2 + c
        for cc in sides(dz):
            put(b.fs.at[dz, cc], fin.at[at], b.fin_s, b.fin_r.at[at], dict(z=flip(z, dz), c=cc))
        if dz == 0:
            get(b.fs.at[0, c], fin.at[at], b.fin_l)

    multiply(0)
    passed(0)
    fd.forward(0)
    fd.forward(1)
    second(0)
    fd.forward(2)
    fetch(fd, 1, 1)
    load_o(1)
    fetch(fd, 2, 0)
    load_o(2)
    multiply(1)
    multiply(2)
    passed(1)
    for g in range(len(GROUPS)):
        fd.last(g)
    fo.last()
    fetch(fd, 3, 1)
    load_o(3)
    passed(2)
    multiply(3)
    second(1)
    passed(3)
    second(2)
    third(0)
    third(1)
    second(3)
    third(2)
    third(3)

    for dz in AWAY + (0,):
        for cc in sides(dz):
            at = flip(z, dz) * NC + cc
            drain(fin.at[at], b.fin_r.at[at])
    drain(fin.at[0], b.fin_l)

    some, tile = first(NR - 1), first(TILE)
    for k in RING:
        drain(b.hnT.at[some, 0, :, tile], b.ag_s.at[NC * k])
        drain(b.hnT.at[some, :, :, tile], b.ag_s.at[NC * k + 1])
    for h in range(NC):
        drain(b.S.at[h, first(NJ - 1)], b.s_s.at[h])
    drain(b.F.at[first(NG - 1)], b.f_s)
    drain(b.q_in.at[first(NJ - 1)], b.q_s)
    drain(b.kv_in.at[1], b.kv_s)
    drain(b.o_in.at[first(NJ - 1)], b.o_s)
    for dz in ORDER:
        if dz:
            sent(dz)
        drain(b.a2.at[dz], b.a2s.at[dz])
        drain(b.b2.at[dz], b.b2s.at[dz])
    drain(fin.at[first(NG - 1)], b.fin_s)
    for f in (fq, fg, fu, fd, fo):
        f.finish()
    for ref in (b.kc, b.vc):
        drain(ref, b.out_l)


def finish(fin, kc_h, vc_h, out, kc_o, vc_o, fin_v, kc, vc, ov, sem):
    get(fin, fin_v, sem.at[0])
    get(kc_h, kc, sem.at[1])
    get(vc_h, vc, sem.at[2])
    drain(fin_v, sem.at[0])
    row_low = lax.broadcasted_iota(jnp.int32, (FEATS, LANE), 1) < HALF
    for zz in RING:
        for p in range(NG):
            lo, hi = (fin_v[zz * NC + cc, :, pl.ds(p * LANE, LANE)].astype(F32) for cc in range(NC))
            pair = [jnp.where(row_low, lo, pltpu.roll(hi, HALF, 1)), jnp.where(row_low, pltpu.roll(lo, HALF, 1), hi)]
            ov[:, pl.ds(zz * NC * ROWS + p * TILE, TILE)] = jnp.concatenate(pair, axis=1).astype(BF16)
    drain(kc, sem.at[1])
    get(kc, kc_o, sem.at[1])
    drain(vc, sem.at[2])
    get(vc, vc_o, sem.at[2])
    get(ov, out, sem.at[0])
    for i, ref in enumerate((ov, kc, vc)):
        drain(ref, sem.at[i])


def solution(mesh):
    inner = Mesh(mesh.devices.reshape(4, 4, 4, 2), tuple('zyxc'))

    def layer(residual, ln_scale, w_query, w_key, w_value, w_gate, w_up, w_out, w_down, k_cache, v_cache, lengths):
        hbm = pl.BlockSpec(memory_space=pltpu.HBM)
        vmem = pl.BlockSpec(memory_space=pltpu.VMEM)
        smem = pl.BlockSpec(memory_space=pltpu.SMEM)
        shape = lambda a: jax.ShapeDtypeStruct(*a)
        results = [((FEATS, BATCH), BF16), (k_cache.shape, BF16), (v_cache.shape, BF16)]
        fin = ((NG, FEATS, ROWS), BF16)
        outs = [fin] + results[1:] + list(HBM_BUFS.values())
        got = pl.pallas_call(
            kernel,
            out_shape=[shape(a) for a in outs],
            in_specs=[hbm, vmem, smem] + [hbm] * 9,
            out_specs=[hbm] * len(outs),
            scratch_shapes=[pltpu.VMEM(*a) for a in VMEM_BUFS.values()] + [DMA(s) if s else DMA for s in SEMS.values()] + NARROW_SEMS + WIDE_SEMS * 3 + NARROW_SEMS,
            name='decode_layer',
            compiler_params=pltpu.CompilerParams(collective_id=0, has_side_effects=True, vmem_limit_bytes=67043328),
        )(residual.T, ln_scale.reshape(1, FEATS), lengths, w_query, w_key, w_value, w_gate, w_up, w_down.T, w_out.T, k_cache, v_cache)
        out, k_new, v_new = pl.pallas_call(
            finish,
            out_shape=[shape(a) for a in results],
            in_specs=[hbm] * 3,
            out_specs=[hbm] * 3,
            scratch_shapes=[pltpu.VMEM(*a) for a in [fin] + results[1:] + results[:1]] + [DMA((3,))],
            name='finish',
        )(*got[:3])
        return out.T, k_new, v_new

    rc, tx, tyz = tuple('zyxc'), tuple('zy'), tuple('xc')
    cache = P(rc, None, None)
    in_specs = (P(None, rc), P(rc), P(tx, tyz), P(tx, None), P(tx, None), P(tx, tyz), P(tx, tyz), P(tyz, tx), P(tyz, tx), cache, cache, P(rc))
    return jax.shard_map(layer, mesh=inner, in_specs=in_specs, out_specs=(P(None, rc), cache, cache), check_vma=False)
```

time: 322 us -> 257 us (0.80)
  Pallas kernels: 315 us -> 256 us
  local copies, waits for them, and re-layouts: 5.29 us -> 0 us
    pallas_call x1, Pallas kernels: 315 us -> 253 us  [layer(): pl.pallas_call(kernel, out_shape=[shape(a) for a in outs], in_specs=[hbm,...]
    unnamed x5 -> x0, local copies, waits for them, and re-layouts: 5.29 us -> none
where the time goes in v3:
time: 257 us
  Pallas kernels  256 us (100%)
    pallas_call x1, Pallas kernels, layer(): pl.pallas_call(kernel, out_shape=[shape(a) for a in outs], in_specs=[hbm,...  253 us

profile of v3, /device:TPU:1, one launch (start us, length us, event | category | flops | bytes accessed | tf_op | source)
XLA Modules:
  0.0 256.7 jit_solution(4241005328909275491)
XLA Ops:
  0.6 252.9 %decode_layer.1 = (bf16[8,40,1024]{2,1,0:T(8,128)(2,1)}, bf16[64,64,128]{2,1,0:T(8,128)(2,1)}, bf16[64,64,128]{2,1,0:T(8,128)(2,1)}, bf16[8,320,896]{2,1,0:T(8,1...) custom-call(bf16[40,8192]{1,0:T(8,128)(2,1)} %bitcast.6, ...), custom_call_target="tpu_custom_call" | custom-call | tf_op jit(solution)/shard_map/decode_layer/pallas_call | solution.py:703
  253.5 3.0 %finish.1 = (bf16[40,8192]{1,0:T(8,128)(2,1)}, bf16[64,64,128]{2,1,0:T(8,128)(2,1)}, bf16[64,64,128]{2,1,0:T(8,128)(2,1)}) custom-call(bf16[8,40,1024]{2,1,0:T(8,128)(2,1)} %get-tuple-element.9.fin, bf16[64,64,128]{2,1,0:T(8,128)(2,1)} %get-tuple-element.10.kc_h, bf16[64,64,128]{2,1,0:T(8,128)(2,1)} %get-tuple-element.11.vc_h), custom_call_target="tpu_custom_call" | custom-call | tf_op jit(solution)/shard_map/finish/pallas_call | solution.py:712

commit v4 on v3

--- a/solution.py
+++ b/solution.py
@@ -11,18 +11,22 @@
 DMA = pltpu.SemaphoreType.DMA
 F32, BF16 = jnp.float32, jnp.bfloat16
 ROWS, MODEL, FEATS, BATCH = 1024, 5120, 40, 8192
-KB, NB, HB, QB, HD, SUB = 1280, 640, 320, 896, 128, 80
+KB, NB, HB, HD, SUB = 1280, 640, 320, 128, 80
 MINE, SEQ, HEADS, LANE, HALF = 64, 64, 40, 128, 64
 NR, NC, NJ, NG = 4, 2, 16, 8
 X_FIRST = (1,)
 CUT = 512
 TILE = 256
 RING = range(4)
+N0, N1, N2, N3 = RING
 AWAY = (1, 3, 2)
 SIDES = AWAY[:2]
 FORTH, BACK = ((1, 0), (3, 1)), ((3, 0), (1, 1))
 GROUPS = ((0, 1), (1, 2), (2, 4))
+SINGLE = ((0, 1), (1, 2), (2, 3), (3, 4))
 ORDER = (0, 1, 3, 2)
+BOTH = NEAR, FAR = (0, 1)
+TURNED = 2
 PAIRS = tuple(sorted(((dy, dx) for dy in RING for dx in RING if dy or dx), key=lambda p: (p.count(2), 0 not in p, abs(p[0] - p[1]))))
 NT = (((1,), (1,)), ((), ()))
 
@@ -52,49 +56,62 @@
 
 
 class Wide:
-    def __init__(self, land, src, sems, pos):
+    def __init__(self, land, src, sems, pos, groups=GROUPS):
         self.land, self.src = land, src
         self.send, self.yr, self.zr, self.fr, self.dr, self.loc = sems
         self.z, self.y, self.x, self.c = pos
         self.base = self.c * 16
+        self.groups = groups
         self.here = set()
 
     def piece(self, yy):
         return self.src.at[:, pl.ds(pl.multiple_of(yy * NB, LANE), NB)]
 
     def at(self, dz, g, base=None):
-        lo, hi = GROUPS[g]
+        lo, hi = self.groups[g]
         return self.land.at[pl.ds((self.base if base is None else base) + dz * 4 + lo, hi - lo)]
 
     def start_local(self):
         get(self.piece(self.y), self.land.at[self.base], self.loc)
 
-    def y_send(self):
-        for dy in AWAY:
+    def y_send(self, order=AWAY):
+        for dy in order:
             yy = flip(self.y, dy)
             put(self.piece(yy), self.land.at[self.base + dy], self.send, self.yr.at[dy - 1], dict(y=yy))
 
     def z_send(self, g):
+        self.wait_y(g)
+        for dz in SIDES:
+            self.z_put(g, dz)
+
+    def wait_y(self, g):
         if g:
-            for dy in range(*GROUPS[g]):
+            for dy in range(*self.groups[g]):
                 drain(self.land.at[self.base + dy], self.yr.at[dy - 1])
+        self.d2d(0, g)
+
+    def z_put(self, g, dz):
+        src = self.at(0, g) if g else self.piece(self.y)
+        dst = self.at(dz, g) if g else self.land.at[self.base + dz * 4]
+        put(src, dst, self.send, self.zr.at[dz // 2 * len(self.groups) + g], dict(z=flip(self.z, dz)))
+
+    def arrive(self, dz, g):
+        drain(self.at(dz, g), self.zr.at[dz // 2 * len(self.groups) + g])
+        self.d2d(dz, g)
+
+    def forward(self, g):
+        for dz in SIDES:
+            self.arrive(dz, g)
+        self.pass_on(g)
+
+    def pass_on(self, g, *sides):
         for k, dz in enumerate(SIDES):
-            to = dict(z=flip(self.z, dz))
-            if g:
-                put(self.at(0, g), self.at(dz, g), self.send, self.zr.at[k * 3 + g], to)
-            else:
-                put(self.piece(self.y), self.land.at[self.base + dz * 4], self.send, self.zr.at[k * 3], to)
-        self.d2d(0, g)
-
-    def forward(self, g):
-        for k, dz in enumerate(SIDES):
-            drain(self.at(dz, g), self.zr.at[k * 3 + g])
-        for k, dz in enumerate(SIDES):
-            put(self.half(dz, g, k), self.half(2, g, k), self.send, self.fr.at[g], dict(z=flip(self.z, AWAY[1 - k])))
-            self.d2d(dz, g)
+            src, dst = (self.at(dz, g), self.at(2, g)) if sides else (self.half(dz, g, k), self.half(2, g, k))
+            if dz in (sides or SIDES):
+                put(src, dst, self.send, self.fr.at[g], dict(z=flip(self.z, 4 - dz)))
 
     def half(self, dz, g, k):
-        lo, hi = GROUPS[g]
+        lo, hi = self.groups[g]
         return self.land.at[pl.ds(self.base + dz * 4 + lo, hi - lo), pl.ds(k * HB // 2, HB // 2)]
 
     def last(self, g):
@@ -104,19 +121,25 @@
     def d2d(self, dz, g):
         to = dict(c=1 - self.c)
         if dz or g:
-            put(self.at(dz, g), self.at(dz, g), self.send, self.dr.at[dz * 3 + g], to)
+            put(self.at(dz, g), self.at(dz, g), self.send, self.dr.at[dz * len(self.groups) + g], to)
         else:
             put(self.piece(self.y), self.land.at[self.base], self.send, self.dr.at[0], to)
 
+    def ready(self, dz, g):
+        if (dz, g) not in self.here:
+            if dz == g == 0:
+                drain(self.land.at[self.base], self.loc)
+            drain(self.at(dz, g, 16 - self.base), self.dr.at[dz * len(self.groups) + g])
+        self.here.add((dz, g))
+
     def load(self, dz, tile, sem):
-        if dz not in self.here:
-            if dz == 0:
-                drain(self.land.at[self.base], self.loc)
-            for g in range(len(GROUPS)):
-                drain(self.at(dz, g, 16 - self.base), self.dr.at[dz * 3 + g])
-        self.here.add(dz)
+        for g in range(len(self.groups)):
+            self.ready(dz, g)
+        self.bring(dz, 0, NR, tile, sem)
+
+    def bring(self, dz, lo, n, tile, sem):
         for cc in range(NC):
-            get(self.land.at[pl.ds(cc * 16 + dz * 4, 4)], tile.at[:, :, pl.ds(cc * NB, NB)], sem)
+            get(self.land.at[pl.ds(cc * 16 + dz * NR + lo, n)], tile.at[:, :, pl.ds(cc * NB, NB)], sem)
 
     def finish(self):
         drain(self.land.at[first(31)], self.send)
@@ -227,23 +250,23 @@
             drain(self.moved(2, h), self.recv.at[4 + h])
 
 
-WIDE_SEMS = [DMA, DMA((3,)), DMA((6,)), DMA((3,)), DMA((12,)), DMA]
+WIDE_SEMS, SINGLE_SEMS = ([DMA, DMA((NR - 1,)), DMA((2 * n,)), DMA((n,)), DMA((NR * n,)), DMA] for n in map(len, (GROUPS, SINGLE)))
 NARROW_SEMS = [DMA, DMA, DMA((2,)), DMA((2,)), DMA((5,)), DMA]
 HBM_BUFS = dict(
-    Q=((NG, HB, QB), BF16), G=((NG * NR, HB, NB), BF16), U=((NG * NR, HB, NB), BF16), D=((NG * NR, HB, NB), BF16), O=((NG, HB, NB), BF16),
+    Q=((NG, HB, NB), BF16), G=((NG * NR, HB, NB), BF16), U=((NG * NR, HB, NB), BF16), D=((NG * NR, HB, NB), BF16), O=((NG, HB, NB), BF16),
     hnT=((NR, NR, HB, ROWS), BF16), a1=((NR, NC, HB, CUT), BF16), b1=((NR, NC, NR, SUB, ROWS - CUT), BF16))
 VMEM_BUFS = dict(
     rT=((FEATS, BATCH), BF16), xs=((NG, FEATS, ROWS + LANE), BF16), F=((NG, FEATS, ROWS + LANE), BF16), S=((NC, NJ, 2, CUT), F32),
     hs=((NR, SUB, ROWS), BF16), hn=((NR, ROWS, KB), BF16), wt=((NC, NR, HB, KB), BF16), wo_t=((NC, NC, HB, NB), BF16),
-    gacc=((ROWS, KB), F32), uacc=((ROWS, KB), F32), qout=((NJ, MINE, QB), BF16), q_in=((NJ, MINE, NB), BF16), kv_in=((NC, MINE, 2 * HD), BF16),
+    gacc=((ROWS, KB), F32), uacc=((ROWS, KB), F32), qout=((NJ, MINE, NB), BF16), kvout=((NJ, MINE, 2 * HD), BF16), kvw=((NC, NC, HB, HD), BF16), q_in=((NJ, MINE, NB), BF16), kv_in=((NG, MINE, 2 * HD), BF16),
     q3=((MINE * HEADS, HD), F32), lenb=((MINE, HD), F32), kc=((MINE, SEQ, HD), BF16), vc=((MINE, SEQ, HD), BF16), kn=((MINE, 2 * HD), F32),
     o_v=((MINE, MODEL), BF16), o_in=((NJ, MINE, NB), BF16), act=((ROWS, KB), BF16), sb=((NR - 1, NR, HB, ROWS), BF16),
-    va=((NC, HB, CUT), BF16), vb=((NC, NR, SUB, ROWS - CUT), BF16),
+    va=((NC, NC, HB, CUT), BF16), vb=((NC, NC, NR, SUB, ROWS - CUT), BF16),
     ta=((NR, NC, HB // 2, CUT), BF16), tb=((NR, NC, NR // 2, SUB, ROWS - CUT), BF16), s2a=((NR, HB, CUT), BF16), s2b=((NR, NR, SUB, ROWS - CUT), BF16),
     a2=((NR, NR - 1, SUB, CUT), BF16), b2=((NR, NR - 1, SUB, ROWS - CUT), BF16), fs=((NR, NC, FEATS, ROWS), BF16))
 ONE, EACH, BY_GROUP = (), (NR,), (NG,)
-SEMS = dict(f_s=ONE, fin_l=ONE, s_s=EACH, s_r=EACH, own_l=EACH, q_s=ONE, q_r=ONE, kv_s=ONE, kv_r=ONE, o_s=ONE, o_r=ONE, fin_s=ONE, out_l=ONE,
-            a1s=EACH, a1r=EACH, b1s=EACH, b1r=EACH, a2s=EACH, a2r=EACH, b2s=EACH, b2r=EACH, ag_s=BY_GROUP, ag_r=(NG, NG), tas=EACH, tbs=EACH, tar=BY_GROUP, tbr=BY_GROUP, ld=EACH, wsem=EACH, osem=EACH, vsem=EACH,
+SEMS = dict(f_s=ONE, fin_l=ONE, s_s=EACH, s_r=EACH, own_l=EACH, q_s=ONE, kw_s=ONE, kw_z=ONE, kw_y=ONE, kw_c=EACH, q_r=ONE, kv_s=ONE, kv_r=ONE, o_s=ONE, o_r=ONE, fin_s=ONE, out_l=ONE,
+            a1s=EACH, b1s=EACH, a2s=EACH, a2r=EACH, b2s=EACH, b2r=EACH, ag_s=BY_GROUP, ag_r=(NG, NG), tas=EACH, tbs=EACH, tar=(NR, NC), tbr=(NR, NC), b1r=(NR, NC), a1r=(NR, NC), ld=EACH, wsem=EACH, osem=EACH, vsem=BY_GROUP,
             f_r=(NC, NG), fin_r=BY_GROUP)
 
 
@@ -255,9 +278,9 @@
     for name in list(HBM_BUFS) + list(VMEM_BUFS) + list(SEMS):
         setattr(b, name, rest.pop(0))
     pos = z, y, x, c = tuple(lax.axis_index(a) for a in 'zyxc')
-    flow = lambda kind, land, src: kind(land, src, [rest.pop(0) for _ in WIDE_SEMS], pos)
-    fq = flow(Narrow, b.Q, (wq, wk, wv))
-    fg, fu, fd = flow(Wide, b.G, wg), flow(Wide, b.U, wu), flow(Wide, b.D, wdT)
+    flow = lambda kind, land, src, *more: kind(land, src, [rest.pop(0) for _ in WIDE_SEMS], pos, *more)
+    fq = flow(Narrow, b.Q, (wq,))
+    fg, fu, fd = flow(Wide, b.G, wg), flow(Wide, b.U, wu), flow(Wide, b.D, wdT, SINGLE)
     fo = flow(Narrow, b.O, (woT,))
     me = y * 4 + x
     row_low = lax.broadcasted_iota(jnp.int32, (FEATS, LANE), 1) < HALF
@@ -293,6 +316,18 @@
             for cc in sides(dz):
                 put(b.xs.at[dz * NC + cc, :, wide(h)], b.F.at[dz * NC + c, :, wide(h)], b.f_s, b.f_r.at[h, dz * NC + c], dict(z=flip(z, dz), c=cc))
     b.F[c] = b.xs[c]
+    def kv_half(slot, side):
+        return b.kvw.at[slot, side]
+
+    for side, w in enumerate((wk, wv)):
+        @pl.when((c == side) & (x == 0))
+        def _():
+            get(w, kv_half(0, side), b.kw_z)
+
+        @pl.when((c == side) & (x > 0))
+        def _():
+            zx = lax.rem(z // 2 + x // 2, 2) * 2 + lax.rem(z + x, 2)
+            put(w, kv_half(0, side), b.kw_s, b.kw_z, dict(z=zx))
     fq.z_first()
     fg.z_send(0)
 
@@ -308,6 +343,7 @@
         for dy, dx in PAIRS:
             put(b.S.at[h, me], b.S.at[h, me], b.s_s.at[h], b.s_r.at[h], dict(y=flip(y, dy), x=flip(x, dx)))
     fq.z_second()
+    fo.z_first()
 
     mine = lambda d: pl.ds(pl.multiple_of(flip(x, d) * SUB, 16), SUB)
 
@@ -353,6 +389,9 @@
     two[0].start()
     one[2].forward()
     one[3].forward()
+    drain(kv_half(0, c), b.kw_z)
+    put(kv_half(0, c), kv_half(1, c), b.kw_s, b.kw_y, dict(y=flip(y, 1)))
+    put(kv_half(0, c), kv_half(0, c), b.kw_s, b.kw_c.at[0], dict(c=1 - c))
     fg.y_send()
     one[1].finish()
     two[1].start()
@@ -364,10 +403,12 @@
     one[3].finish()
     fg.z_send(1)
     fq.last()
+    drain(kv_half(1, c), b.kw_y)
+    put(kv_half(1, c), kv_half(1, c), b.kw_s, b.kw_c.at[1], dict(c=1 - c))
 
     def load_q(pair):
         for i in range(NC):
-            fq.load(NC * pair + i, b.sb.at[pair, part(i), :, first(QB)], b.osem.at[pair])
+            fq.load(NC * pair + i, b.sb.at[pair, part(i), :, first(NB)], b.osem.at[pair])
 
     def stage(k):
         two[k].finish()
@@ -382,8 +423,11 @@
 
     def query(k):
         at = pl.ds(k * TILE, TILE)
-        new = sum(jnp.dot(b.hn[dz, at, :NB], b.sb[dz // 2, part(dz % 2), :, :QB].reshape(NB, QB), preferred_element_type=F32) for dz in RING)
-        b.qout[pl.ds(k * NR, NR)] = new.astype(BF16).reshape(NR, MINE, QB)
+        new = sum(jnp.dot(b.hn[dz, at, :NB], b.sb[dz // 2, part(dz % 2), :, :NB].reshape(NB, NB), preferred_element_type=F32) for dz in RING)
+        b.qout[pl.ds(k * NR, NR)] = new.astype(BF16).reshape(NR, MINE, NB)
+        kv = jnp.concatenate([b.kvw[:, side].reshape(NB, HD) for side in range(NC)], axis=1)
+        new = jnp.dot(b.hn[x, at, :NB], kv, preferred_element_type=F32)
+        b.kvout[pl.ds(k * NR, NR)] = new.astype(BF16).reshape(NR, MINE, 2 * HD)
 
     def project(acc, i, slot, lo=0, hi=ROWS, fresh=False, wait=True):
         if wait:
@@ -396,6 +440,18 @@
             acc[at, :] = new if fresh else new + acc[at, :]
 
     fetch = lambda f, i, slot: f.load(ORDER[i], b.wt.at[slot], b.wsem.at[slot])
+
+    def roles(i):
+        return (0, 3, 2, 1) if i == TURNED else tuple(RING)
+
+    def fetch_d(i, *parts):
+        for h in parts:
+            for t in (2 * h, 2 * h + 1):
+                g = roles(i)[t]
+                fd.ready(ORDER[i], g)
+                fd.bring(ORDER[i], g, 1, b.wt.at[i % 2, pl.ds(t, 1)], b.wsem.at[2 * h + i % 2])
+
+
     fg.z_send(2)
     fu.z_send(0)
     load_q(0)
@@ -405,7 +461,9 @@
     two[3].start()
     turn(0)
     for pair in range(NC):
-        drain(b.sb.at[pair, :, :, first(QB)], b.osem.at[pair])
+        drain(b.sb.at[pair, :, :, first(NB)], b.osem.at[pair])
+    for slot in range(NC):
+        drain(kv_half(slot, 1 - c), b.kw_c.at[slot])
     query(0)
     two[1].forward()
     fu.y_send()
@@ -430,14 +488,17 @@
     turn(3)
     fetch(fg, 0, 1)
     query(3)
+    for dy in (0, 2):
+        for dx in AWAY + (0,)[:dy]:
+            yy, xx = flip(y, dy), flip(x, dx)
+            put(b.kvout.at[yy * NR + xx], b.kv_in.at[2 * dy + x], b.kv_s, b.kv_r, dict(y=yy, x=xx))
     for dy, dx in PAIRS:
         yy, xx = flip(y, dy), flip(x, dx)
-        put(b.qout.at[yy * NR + xx, :, first(NB)], b.q_in.at[me], b.q_s, b.q_r, dict(y=yy, x=xx))
-    put(b.qout.at[flip(y, 2) * NR + x, :, pl.ds(NB, 2 * HD)], b.kv_in.at[1], b.kv_s, b.kv_r, dict(y=flip(y, 2)))
-    b.q_in[me] = b.qout[me, :, :NB]
-    b.kv_in[0] = b.qout[me, :, NB:]
+        put(b.qout.at[yy * NR + xx], b.q_in.at[me], b.q_s, b.q_r, dict(y=yy, x=xx))
+    b.q_in[me] = b.qout[me]
+    b.kv_in[x] = b.kvout[me]
     fo.start()
-    fd.y_send()
+    fd.y_send((2, 1, 3))
 
     project(b.gacc, 1, 0, 3 * TILE, ROWS, fresh=True, wait=False)
     fetch(fg, 2, 0)
@@ -453,7 +514,7 @@
     drain(b.kc, b.ld.at[1])
     drain(b.vc, b.ld.at[2])
     drain(b.q_in.at[first(NJ - 1)], b.q_r)
-    drain(b.kv_in.at[1], b.kv_r)
+    drain(b.kv_in.at[first(NG - 1)], b.kv_r)
 
     @pl.loop(0, MINE)
     def _(r):
@@ -464,7 +525,7 @@
     cos = jnp.cos(angle)
     sin = jnp.where(low, -jnp.sin(angle), jnp.sin(angle))
     rope = lambda v: v * cos + pltpu.roll(v, HALF, 1) * sin
-    kv = (b.kv_in[0].astype(F32) + b.kv_in[1].astype(F32)).astype(BF16).astype(F32)
+    kv = sum(b.kv_in[i].astype(F32) for i in range(NG)).astype(BF16).astype(F32)
     b.kn[:, :HD] = rope(kv[:, :HD])
     b.kn[:, HD:] = kv[:, HD:]
     for xs in RING:
@@ -475,33 +536,28 @@
     t_row = lax.broadcasted_iota(jnp.int32, (SEQ, HD), 0)
     t_col = lax.broadcasted_iota(jnp.int32, (HEADS, SEQ), 1)
 
-    def attend(r):
-        here = t_row == lens[r]
-        new = b.kn[pl.ds(r, 1), :]
-        keys = jnp.where(here, new[:, :HD].astype(BF16).astype(F32), b.kc[r].astype(F32)).astype(BF16)
-        vals = jnp.where(here, new[:, HD:], b.vc[r].astype(F32)).astype(BF16)
-        b.kc[r] = keys
-        b.vc[r] = vals
-        at = pl.ds(pl.multiple_of(r * HEADS, 8), HEADS)
-        s = lax.dot_general(b.q3[at, :].astype(BF16), keys, NT, preferred_element_type=F32) * (HD ** -0.5)
-        s = jnp.where(t_col <= lens[r], s, -1e30)
-        e = jnp.exp(s - jnp.max(s, axis=1, keepdims=True))
-        p = (e / jnp.sum(e, axis=1, keepdims=True)).astype(BF16)
-        b.q3[at, :] = jnp.dot(p, vals, preferred_element_type=F32)
+    def attend(rows):
+        ats = [pl.ds(pl.multiple_of(r * HEADS, 8), HEADS) for r in rows]
+        here = [t_row == lens[r] for r in rows]
+        new = [b.kn[pl.ds(r, 1), :] for r in rows]
+        keys = [jnp.where(h, n[:, :HD].astype(BF16).astype(F32), b.kc[r].astype(F32)).astype(BF16) for r, h, n in zip(rows, here, new)]
+        vals = [jnp.where(h, n[:, HD:], b.vc[r].astype(F32)).astype(BF16) for r, h, n in zip(rows, here, new)]
+        s = [lax.dot_general(b.q3[at, :].astype(BF16), k, NT, preferred_element_type=F32) for at, k in zip(ats, keys)]
+        s = [jnp.where(t_col <= lens[r], v * (HD ** -0.5), -1e30) for r, v in zip(rows, s)]
+        top = [jnp.max(v, axis=1, keepdims=True) for v in s]
+        e = [jnp.exp(v - t) for v, t in zip(s, top)]
+        total = [jnp.sum(v, axis=1, keepdims=True) for v in e]
+        p = [(v / t).astype(BF16) for v, t in zip(e, total)]
+        o = [jnp.dot(v, w, preferred_element_type=F32) for v, w in zip(p, vals)]
+        for r, at, k, v, w in zip(rows, ats, keys, vals, o):
+            b.kc[r], b.vc[r], b.q3[at, :] = k, v, w
 
     def attend_some(lo, hi):
-        @pl.loop(lo // NR, hi // NR)
+        @pl.loop(lo // NG, hi // NG)
         def _(step):
-            for k in RING:
-                attend(step * NR + k)
-
-    attend_some(0, MINE // 4)
-    fu.forward(2)
-    fo.z_first()
-    fo.z_second()
-    fd.z_send(0)
-    fd.z_send(1)
-    attend_some(MINE // 4, MINE)
+            attend([step * NG + k for k in range(NG)])
+
+    attend_some(0, MINE)
     get(b.kc, kc_o, b.out_l)
     get(b.vc, vc_o, b.out_l)
     for h in range(HEADS):
@@ -512,134 +568,212 @@
         put(block(yy, xx), b.o_in.at[me], b.o_s, b.o_r, dict(y=yy, x=xx))
     b.o_in[me] = block(y, x)[...]
 
-    fd.z_send(2)
+    def start_d(*plan):
+        for g, planes in plan:
+            fd.wait_y(g)
+            for dz in planes:
+                fd.z_put(g, dz)
+
+    fu.forward(2)
+    fo.z_second()
     fetch(fu, 1, 1)
     fetch(fu, 2, 0)
     project(b.uacc, 1, 1)
+    project(b.uacc, 2, 0)
+    start_d((2, SIDES))
     fu.last(0)
     fu.last(1)
     fu.last(2)
-    project(b.uacc, 2, 0)
     fetch(fu, 3, 1)
-    fetch(fd, 0, 0)
     load_o = lambda i: fo.load(ORDER[i], b.wo_t.at[i % 2], b.osem.at[i % 2])
+    start_d((1, SIDES[1:]), (3, SIDES[:1]), (0, SIDES))
+    project(b.uacc, 3, 1)
+    fetch_d(0, *BOTH)
     load_o(0)
-    project(b.uacc, 3, 1)
 
     @pl.loop(0, ROWS // LANE)
     def _(r):
         at = pl.ds(pl.multiple_of(r * LANE, LANE), LANE)
         g = b.gacc[at, :].astype(BF16).astype(F32)
         b.act[at, :] = (g / (1.0 + jnp.exp(-g)) * b.uacc[at, :].astype(BF16).astype(F32)).astype(BF16)
-    fo.forward()
-
-    drain(b.o_in.at[first(NJ - 1)], b.o_r)
+    drain(b.o_in.at[first(NJ - N1)], b.o_r)
     HA, HBk = first(CUT), pl.ds(CUT, ROWS - CUT)
 
-    def sent(dz):
+    rows_of = lambda h: pl.ds(h * HB // N2, HB // N2)
+
+    def sent(i):
         for land, sem in ((b.a1, b.a1s), (b.b1, b.b1s), (b.ta, b.tas), (b.tb, b.tbs)):
-            drain(land.at[dz], sem.at[dz])
-
-    def multiply(i):
-        dz, slot = ORDER[i], i % 2
-        drain(b.wt.at[slot], b.wsem.at[slot])
-        drain(b.wo_t.at[slot], b.osem.at[slot])
-        if i == 3:
-            sent(ORDER[0])
+            drain(land.at[i], sem.at[i])
+
+    def multiply(i, h):
+        slot, k, tall = i % N2, i % N3, part(h)
+        drain(b.wt.at[slot, tall], b.wsem.at[N2 * h + slot])
+        heads = [t for t in (N2 * h, N2 * h + N1) if roles(i)[t] < N2]
+        if heads and i not in loaded_o:
+            drain(b.wo_t.at[slot], b.osem.at[slot])
+            loaded_o.add(i)
 
         def some(lo, hi):
             @pl.loop(lo // TILE, hi // TILE)
             def _(r):
                 at = pl.ds(pl.multiple_of(r * TILE, TILE), TILE)
-                out = lax.dot_general(b.wt[slot].reshape(KB, KB), b.act[at, :], NT, preferred_element_type=F32)
-                rows = b.o_in[pl.ds(r * 4, 4)].reshape(TILE, NB)
-                att = lax.dot_general(b.wo_t[slot].reshape(NB, NB), rows, NT, preferred_element_type=F32)
-                b.sb[i % 3, first(2), :, at] = (out[:NB] + att).astype(BF16).reshape(2, HB, TILE)
-                b.sb[i % 3, pl.ds(2, 2), :, at] = out[NB:].astype(BF16).reshape(2, HB, TILE)
-
-        some(0, CUT)
-        half = HB // 2
-        for d, h in FORTH:
-            rows = pl.ds(h * half, half)
-            put(b.sb.at[i % 3, 2, rows, HA], b.ta.at[dz, h], b.tas.at[dz], b.tar.at[2 * dz + h], dict(y=flip(y, d)))
-            put(b.sb.at[i % 3, d, rows, HA], b.a1.at[dz, h, rows], b.a1s.at[dz], b.a1r.at[dz], dict(y=flip(y, d)))
-        some(CUT, ROWS)
-        for d, h in FORTH:
-            dys = pl.ds(2 * h, 2)
-            put(b.sb.at[i % 3, dys, mine(2), HBk], b.tb.at[dz, h], b.tbs.at[dz], b.tbr.at[2 * dz + h], dict(x=flip(x, d)))
-            put(b.sb.at[i % 3, dys, mine(d), HBk], b.b1.at[dz, h, dys], b.b1s.at[dz], b.b1r.at[dz], dict(x=flip(x, d)))
-
-    def passed(i):
-        dz, slot = ORDER[i], i % 3
-        half = HB // 2
-        for d, h in BACK:
-            rows = pl.ds(h * half, half)
-            drain(b.ta.at[dz, h], b.tar.at[2 * dz + h])
-            b.sb[slot, d, rows, HA] = (b.sb[slot, d, rows, HA].astype(F32) + b.ta[dz, h].astype(F32)).astype(BF16)
-            put(b.sb.at[slot, d, rows, HA], b.a1.at[dz, 1 - h, rows], b.a1s.at[dz], b.a1r.at[dz], dict(y=flip(y, d)))
-        for d, h in BACK:
-            dys = pl.ds(2 * h, 2)
-            drain(b.tb.at[dz, h], b.tbr.at[2 * dz + h])
-            b.sb[slot, dys, mine(d), HBk] = (b.sb[slot, dys, mine(d), HBk].astype(F32) + b.tb[dz, h].astype(F32)).astype(BF16)
-            put(b.sb.at[slot, dys, mine(d), HBk], b.b1.at[dz, 1 - h, dys], b.b1s.at[dz], b.b1r.at[dz], dict(x=flip(x, d)))
-
-    def second(i):
-        dz, slot = ORDER[i], i % 3
-        drain(b.a1.at[dz], b.a1r.at[dz])
-        get(b.a1.at[dz], b.va, b.vsem.at[0])
-        drain(b.b1.at[dz], b.b1r.at[dz])
-        get(b.b1.at[dz], b.vb, b.vsem.at[1])
-        drain(b.va, b.vsem.at[0])
-        b.s2a[dz] = (b.sb[slot, 0, :, HA].astype(F32) + (b.va[0].astype(F32) + b.va[1].astype(F32))).astype(BF16)
+                out = lax.dot_general(b.wt[slot, tall].reshape(NB, KB), b.act[at, :], NT, preferred_element_type=F32)
+                rows = b.o_in[pl.ds(r * NR, NR)].reshape(TILE, NB)
+                if len(heads) == N2:
+                    out += lax.dot_general(b.wo_t[slot].reshape(NB, NB), rows, NT, preferred_element_type=F32)
+                elif heads:
+                    more = lax.dot_general(b.wo_t[slot, roles(i)[heads[N0]]], rows, NT, preferred_element_type=F32)
+                    halves = [out[:HB], out[HB:]]
+                    halves[heads[N0] - N2 * h] += more
+                    out = jnp.concatenate(halves, axis=N0)
+                b.sb[k, tall, :, at] = out.astype(BF16).reshape(N2, HB, TILE)
+
+        def first_rows():
+            some(N0, CUT)
+            if h == FAR:
+                for j, d in enumerate(ends(i)):
+                    put(b.sb.at[k, N2, rows_of(j), HA], b.ta.at[i, j], b.tas.at[i], b.tar.at[i, j], dict(y=flip(y, d)))
+            put(b.sb.at[k, SIDES[h], rows_of(h), HA], b.a1.at[i, h, rows_of(h)], b.a1s.at[i], b.a1r.at[i, h], dict(y=flip(y, ends(i)[h])))
+            if h == NEAR and i:
+                pass_a(i, h)
+
+        def last_rows():
+            some(CUT, ROWS)
+            d = ends(i)[h]
+            put(b.sb.at[k, tall, mine(N2), HBk], b.tb.at[i, h], b.tbs.at[i], b.tbr.at[i, h], dict(x=flip(x, d)))
+            put(b.sb.at[k, tall, mine(d), HBk], b.b1.at[i, h, tall], b.b1s.at[i], b.b1r.at[i, h], dict(x=flip(x, d)))
+
+        for step in (first_rows, last_rows)[::N1 if h else -N1]:
+            step()
+
+    loaded_o = set()
+    ends = lambda i: SIDES[::-N1] if i == TURNED else SIDES
+
+    def pass_a(i, h):
+        k, t, rows = i % N3, SIDES[h], rows_of(N1 - h)
+        drain(b.ta.at[i, N1 - h], b.tar.at[i, N1 - h])
+        b.sb[k, t, rows, HA] = (b.sb[k, t, rows, HA].astype(F32) + b.ta[i, N1 - h].astype(F32)).astype(BF16)
+        put(b.sb.at[k, t, rows, HA], b.a1.at[i, h, rows], b.a1s.at[i], b.a1r.at[i, h], dict(y=flip(y, ends(i)[h])))
+
+    def passed(i, h):
+        k, tall = i % N3, part(h)
+        if h == FAR or i == N0:
+            pass_a(i, h)
+        d = ends(i)[N1 - h]
+        drain(b.tb.at[i, h], b.tbr.at[i, h])
+        b.sb[k, tall, mine(d), HBk] = (b.sb[k, tall, mine(d), HBk].astype(F32) + b.tb[i, h].astype(F32)).astype(BF16)
+        put(b.sb.at[k, tall, mine(d), HBk], b.b1.at[i, N1 - h, tall], b.b1s.at[i], b.b1r.at[i, h], dict(x=flip(x, d)))
+
+    def load_a(i):
+        for k in range(NC):
+            drain(b.a1.at[i, k], b.a1r.at[i, k])
+        get(b.a1.at[i], b.va.at[i % N2], b.vsem.at[i % N2])
+
+    def second_a(i):
+        dz, va = ORDER[i], b.va.at[i % N2]
+        drain(va, b.vsem.at[i % N2])
+        b.s2a[dz] = (b.sb[i % N3, N0, :, HA].astype(F32) + (va[N0].astype(F32) + va[N1].astype(F32))).astype(BF16)
         for d in AWAY:
-            put(b.s2a.at[dz, mine(d)], b.a2.at[dz, d - 1], b.a2s.at[dz], b.a2r.at[dz], dict(x=flip(x, d)))
-        drain(b.vb, b.vsem.at[1])
-        b.s2b[dz] = (b.sb[slot, :, mine(0), HBk].astype(F32) + (b.vb[0].astype(F32) + b.vb[1].astype(F32))).astype(BF16)
-        for d in AWAY:
-            put(b.s2b.at[dz, d], b.b2.at[dz, d - 1], b.b2s.at[dz], b.b2r.at[dz], dict(y=flip(y, d)))
+            put(b.s2a.at[dz, mine(d)], b.a2.at[dz, d - N1], b.a2s.at[dz], b.a2r.at[dz], dict(x=flip(x, d)))
+
+    def load_b(i, h):
+        drain(b.b1.at[i, :, part(h)], b.b1r.at[i, h])
+        get(b.b1.at[i, :, part(h)], b.vb.at[i % N2, :, part(h)], b.vsem.at[N2 + N2 * h + i % N2])
+
+    def second_b(i, h):
+        k, tall = i % N3, part(h)
+        vb = b.vb.at[i % N2, :, tall]
+        drain(vb, b.vsem.at[N2 + N2 * h + i % N2])
+        b.s2b[i, tall] = (b.sb[k, tall, mine(N0), HBk].astype(F32) + (vb[N0].astype(F32) + vb[N1].astype(F32))).astype(BF16)
+        for t in ((N1,), (N3, N2))[h]:
+            put(b.s2b.at[i, t], b.b2.at[i, t - N1], b.b2s.at[i], b.b2r.at[i], dict(y=flip(y, roles(i)[t])))
 
     def third(i):
         dz = ORDER[i]
         drain(b.a2.at[dz], b.a2r.at[dz])
-        drain(b.b2.at[dz], b.b2r.at[dz])
-        for src, own, lanes, shifted in ((b.a2, b.s2a[dz, mine(0)], HA, pl.ds(LANE, CUT)), (b.b2, b.s2b[dz, 0], HBk, pl.ds(LANE + CUT, ROWS - CUT))):
-            total = own.astype(F32) + added(src.at[dz])
+        drain(b.b2.at[i], b.b2r.at[i])
+        for src, own, lanes, at in ((b.a2.at[dz], b.s2a[dz, mine(N0)], HA, LANE), (b.b2.at[i], b.s2b[i, N0], HBk, LANE + CUT)):
+            total = own.astype(F32) + sum(src[d].astype(F32) for d in range(NR - N1))
             for cc in range(NC):
-                b.fs[dz, cc, :, lanes] = (b.F[dz * 2 + cc, :, shifted].astype(F32) + total[cc * FEATS:(cc + 1) * FEATS]).astype(BF16)
-        at = z * 2 + c
+                b.fs[dz, cc, :, lanes] = (b.F[dz * NC + cc, :, pl.ds(at, CUT)].astype(F32) + total[cc * FEATS:(cc + N1) * FEATS]).astype(BF16)
+        at = z * NC + c
         for cc in sides(dz):
             put(b.fs.at[dz, cc], fin.at[at], b.fin_s, b.fin_r.at[at], dict(z=flip(z, dz), c=cc))
-        if dz == 0:
-            get(b.fs.at[0, c], fin.at[at], b.fin_l)
-
-    multiply(0)
-    passed(0)
-    fd.forward(0)
-    fd.forward(1)
-    second(0)
-    fd.forward(2)
-    fetch(fd, 1, 1)
-    load_o(1)
-    fetch(fd, 2, 0)
-    load_o(2)
-    multiply(1)
-    multiply(2)
-    passed(1)
-    for g in range(len(GROUPS)):
-        fd.last(g)
+        if dz == N0:
+            get(b.fs.at[N0, c], fin.at[at], b.fin_l)
+
+    multiply(N0, FAR)
+    multiply(N0, NEAR)
+    for dz, g in ((N1, N2), (N3, N2), (N1, N3), (N3, N1)):
+        fd.arrive(dz, g)
+    fd.pass_on(N2)
+    fd.pass_on(N3, N1)
+    fd.pass_on(N1, N3)
+    fd.z_put(N1, N1)
+    fd.z_put(N3, N3)
+    fo.forward()
+    fetch_d(N1, FAR)
+    load_o(N2)
+    fetch_d(N2, FAR)
+    passed(N0, FAR)
+    passed(N0, NEAR)
+    multiply(N1, FAR)
+    multiply(N2, FAR)
+    load_b(N0, FAR)
+    load_a(N0)
+    load_b(N0, NEAR)
+    second_b(N0, FAR)
+    second_a(N0)
+    second_b(N0, NEAR)
+    passed(N1, FAR)
+    passed(N2, FAR)
+    load_o(N1)
+    fd.last(N2)
+    fd.last(N3)
+    fd.last(N1)
+    sent(N0)
+    fetch_d(N3, FAR)
+    multiply(N3, FAR)
+    load_b(N1, FAR)
+    load_b(N2, FAR)
+    second_b(N1, FAR)
+    second_b(N2, FAR)
+    fd.arrive(N1, N0)
+    fd.arrive(N3, N0)
+    fd.pass_on(N0)
+    fd.arrive(N1, N1)
+    fd.arrive(N3, N3)
+    fetch_d(N1, NEAR)
+    fetch_d(N2, NEAR)
+    multiply(N1, NEAR)
+    multiply(N2, NEAR)
+    passed(N3, FAR)
     fo.last()
-    fetch(fd, 3, 1)
-    load_o(3)
-    passed(2)
-    multiply(3)
-    second(1)
-    passed(3)
-    second(2)
-    third(0)
-    third(1)
-    second(3)
-    third(2)
-    third(3)
+    fd.last(N0)
+    fetch_d(N3, NEAR)
+    load_o(N3)
+    multiply(N3, NEAR)
+    passed(N1, NEAR)
+    passed(N2, NEAR)
+    load_b(N3, FAR)
+    load_a(N1)
+    load_a(N2)
+    second_b(N3, FAR)
+    second_a(N1)
+    second_a(N2)
+    passed(N3, NEAR)
+    load_b(N1, NEAR)
+    load_b(N2, NEAR)
+    second_b(N1, NEAR)
+    second_b(N2, NEAR)
+    third(N0)
+    load_a(N3)
+    load_b(N3, NEAR)
+    second_a(N3)
+    second_b(N3, NEAR)
+    third(N1)
+    third(N2)
+    third(N3)
 
     for dz in AWAY + (0,):
         for cc in sides(dz):
@@ -655,7 +789,13 @@
         drain(b.S.at[h, first(NJ - 1)], b.s_s.at[h])
     drain(b.F.at[first(NG - 1)], b.f_s)
     drain(b.q_in.at[first(NJ - 1)], b.q_s)
-    drain(b.kv_in.at[1], b.kv_s)
+    drain(b.kv_in.at[first(NG - 1)], b.kv_s)
+    drain(b.kvw.at[0], b.kw_s)
+    drain(kv_half(1, c), b.kw_s)
+
+    @pl.when(x > 0)
+    def _():
+        drain(kv_half(0, c), b.kw_s)
     drain(b.o_in.at[first(NJ - 1)], b.o_s)
     for dz in ORDER:
         if dz:
@@ -705,7 +845,7 @@
             out_shape=[shape(a) for a in outs],
             in_specs=[hbm, vmem, smem] + [hbm] * 9,
             out_specs=[hbm] * len(outs),
-            scratch_shapes=[pltpu.VMEM(*a) for a in VMEM_BUFS.values()] + [DMA(s) if s else DMA for s in SEMS.values()] + NARROW_SEMS + WIDE_SEMS * 3 + NARROW_SEMS,
+            scratch_shapes=[pltpu.VMEM(*a) for a in VMEM_BUFS.values()] + [DMA(s) if s else DMA for s in SEMS.values()] + NARROW_SEMS + WIDE_SEMS * 2 + SINGLE_SEMS + NARROW_SEMS,
             name='decode_layer',
             compiler_params=pltpu.CompilerParams(collective_id=0, has_side_effects=True, vmem_limit_bytes=67043328),
         )(residual.T, ln_scale.reshape(1, FEATS), lengths, w_query, w_key, w_value, w_gate, w_up, w_down.T, w_out.T, k_cache, v_cache)

time: 257 us -> 253 us (0.984)
  Pallas kernels: 256 us -> 251 us
    pallas_call x1, Pallas kernels: 253 us -> 248 us  [layer(): pl.pallas_call(kernel, out_shape=[shape(a) for a in outs], in_specs=[hbm,...]
where the time goes in v4:
time: 253 us; the launch traced here: 252 us
  Pallas kernels  251 us (99%)
    pallas_call x1, Pallas kernels, layer(): pl.pallas_call(kernel, out_shape=[shape(a) for a in outs], in_specs=[hbm,...  248 us

profile of v4, /device:TPU:1, one launch (start us, length us, event | category | flops | bytes accessed | tf_op | source)
XLA Modules:
  0.0 252.1 jit_solution(6186947101624225929)
XLA Ops:
  0.6 248.3 %decode_layer.1 = (bf16[8,40,1024]{2,1,0:T(8,128)(2,1)}, bf16[64,64,128]{2,1,0:T(8,128)(2,1)}, bf16[64,64,128]{2,1,0:T(8,128)(2,1)}, bf16[8,320,640]{2,1,0:T(8,1...) custom-call(bf16[40,8192]{1,0:T(8,128)(2,1)} %bitcast.6, ...), custom_call_target="tpu_custom_call" | custom-call | tf_op jit(solution)/shard_map/decode_layer/pallas_call | solution.py:843
  249.0 3.0 %finish.1 = (bf16[40,8192]{1,0:T(8,128)(2,1)}, bf16[64,64,128]{2,1,0:T(8,128)(2,1)}, bf16[64,64,128]{2,1,0:T(8,128)(2,1)}) custom-call(bf16[8,40,1024]{2,1,0:T(8,128)(2,1)} %get-tuple-element.9.fin, bf16[64,64,128]{2,1,0:T(8,128)(2,1)} %get-tuple-element.10.kc_h, bf16[64,64,128]{2,1,0:T(8,128)(2,1)} %get-tuple-element.11.vc_h), custom_call_target="tpu_custom_call" | custom-call | tf_op jit(solution)/shard_map/finish/pallas_call | solution.py:852

commit v5 on v4

--- a/solution.py
+++ b/solution.py
@@ -586,8 +586,8 @@
     fu.last(2)
     fetch(fu, 3, 1)
     load_o = lambda i: fo.load(ORDER[i], b.wo_t.at[i % 2], b.osem.at[i % 2])
+    project(b.uacc, 3, 1)
     start_d((1, SIDES[1:]), (3, SIDES[:1]), (0, SIDES))
-    project(b.uacc, 3, 1)
     fetch_d(0, *BOTH)
     load_o(0)
 

time: 253 us -> 251 us (level)
  no operation moved by 1% of the time
where the time goes in v5:
time: 251 us
  Pallas kernels  250 us (100%)
    pallas_call x1, Pallas kernels, layer(): pl.pallas_call(kernel, out_shape=[shape(a) for a in outs], in_specs=[hbm,...  247 us

profile of v5, /device:TPU:1, one launch (start us, length us, event | category | flops | bytes accessed | tf_op | source)
XLA Modules:
  0.0 250.7 jit_solution(16330750661152554030)
XLA Ops:
  0.6 246.9 %decode_layer.1 = (bf16[8,40,1024]{2,1,0:T(8,128)(2,1)}, bf16[64,64,128]{2,1,0:T(8,128)(2,1)}, bf16[64,64,128]{2,1,0:T(8,128)(2,1)}, bf16[8,320,640]{2,1,0:T(8,1...) custom-call(bf16[40,8192]{1,0:T(8,128)(2,1)} %bitcast.6, ...), custom_call_target="tpu_custom_call" | custom-call | tf_op jit(solution)/shard_map/decode_layer/pallas_call | solution.py:843
  247.6 3.0 %finish.1 = (bf16[40,8192]{1,0:T(8,128)(2,1)}, bf16[64,64,128]{2,1,0:T(8,128)(2,1)}, bf16[64,64,128]{2,1,0:T(8,128)(2,1)}) custom-call(bf16[8,40,1024]{2,1,0:T(8,128)(2,1)} %get-tuple-element.9.fin, bf16[64,64,128]{2,1,0:T(8,128)(2,1)} %get-tuple-element.10.kc_h, bf16[64,64,128]{2,1,0:T(8,128)(2,1)} %get-tuple-element.11.vc_h), custom_call_target="tpu_custom_call" | custom-call | tf_op jit(solution)/shard_map/finish/pallas_call | solution.py:852

commit v6 on v5

--- a/solution.py
+++ b/solution.py
@@ -706,11 +706,11 @@
     multiply(N0, NEAR)
     for dz, g in ((N1, N2), (N3, N2), (N1, N3), (N3, N1)):
         fd.arrive(dz, g)
+    fd.z_put(N1, N1)
+    fd.z_put(N3, N3)
     fd.pass_on(N2)
     fd.pass_on(N3, N1)
     fd.pass_on(N1, N3)
-    fd.z_put(N1, N1)
-    fd.z_put(N3, N3)
     fo.forward()
     fetch_d(N1, FAR)
     load_o(N2)
@@ -726,18 +726,7 @@
     second_a(N0)
     second_b(N0, NEAR)
     passed(N1, FAR)
-    passed(N2, FAR)
     load_o(N1)
-    fd.last(N2)
-    fd.last(N3)
-    fd.last(N1)
-    sent(N0)
-    fetch_d(N3, FAR)
-    multiply(N3, FAR)
-    load_b(N1, FAR)
-    load_b(N2, FAR)
-    second_b(N1, FAR)
-    second_b(N2, FAR)
     fd.arrive(N1, N0)
     fd.arrive(N3, N0)
     fd.pass_on(N0)
@@ -746,30 +735,41 @@
     fetch_d(N1, NEAR)
     fetch_d(N2, NEAR)
     multiply(N1, NEAR)
+    passed(N2, FAR)
     multiply(N2, NEAR)
-    passed(N3, FAR)
+    fd.last(N2)
+    fd.last(N3)
+    fd.last(N1)
+    sent(N0)
+    fetch_d(N3, FAR)
+    multiply(N3, FAR)
+    passed(N1, NEAR)
+    passed(N2, NEAR)
+    load_b(N1, FAR)
+    load_b(N2, FAR)
+    second_b(N1, FAR)
+    second_b(N2, FAR)
     fo.last()
     fd.last(N0)
     fetch_d(N3, NEAR)
     load_o(N3)
+    passed(N3, FAR)
     multiply(N3, NEAR)
-    passed(N1, NEAR)
-    passed(N2, NEAR)
-    load_b(N3, FAR)
     load_a(N1)
     load_a(N2)
-    second_b(N3, FAR)
     second_a(N1)
     second_a(N2)
-    passed(N3, NEAR)
     load_b(N1, NEAR)
     load_b(N2, NEAR)
     second_b(N1, NEAR)
     second_b(N2, NEAR)
+    passed(N3, NEAR)
     third(N0)
+    load_b(N3, FAR)
+    second_b(N3, FAR)
     load_a(N3)
+    second_a(N3)
     load_b(N3, NEAR)
-    second_a(N3)
     second_b(N3, NEAR)
     third(N1)
     third(N2)

time: 251 us -> 248 us (0.988)
  Pallas kernels: 250 us -> 247 us
    pallas_call x1, Pallas kernels: 247 us -> 244 us  [layer(): pl.pallas_call(kernel, out_shape=[shape(a) for a in outs], in_specs=[hbm,...]
where the time goes in v6:
time: 248 us
  Pallas kernels  247 us (100%)
    pallas_call x1, Pallas kernels, layer(): pl.pallas_call(kernel, out_shape=[shape(a) for a in outs], in_specs=[hbm,...  244 us

profile of v6, /device:TPU:1, one launch (start us, length us, event | category | flops | bytes accessed | tf_op | source)
XLA Modules:
  0.0 247.8 jit_solution(1121157444732542533)
XLA Ops:
  0.6 244.0 %decode_layer.1 = (bf16[8,40,1024]{2,1,0:T(8,128)(2,1)}, bf16[64,64,128]{2,1,0:T(8,128)(2,1)}, bf16[64,64,128]{2,1,0:T(8,128)(2,1)}, bf16[8,320,640]{2,1,0:T(8,1...) custom-call(bf16[40,8192]{1,0:T(8,128)(2,1)} %bitcast.6, ...), custom_call_target="tpu_custom_call" | custom-call | tf_op jit(solution)/shard_map/decode_layer/pallas_call | solution.py:843
  244.6 3.0 %finish.1 = (bf16[40,8192]{1,0:T(8,128)(2,1)}, bf16[64,64,128]{2,1,0:T(8,128)(2,1)}, bf16[64,64,128]{2,1,0:T(8,128)(2,1)}) custom-call(bf16[8,40,1024]{2,1,0:T(8,128)(2,1)} %get-tuple-element.9.fin, bf16[64,64,128]{2,1,0:T(8,128)(2,1)} %get-tuple-element.10.kc_h, bf16[64,64,128]{2,1,0:T(8,128)(2,1)} %get-tuple-element.11.vc_h), custom_call_target="tpu_custom_call" | custom-call | tf_op jit(solution)/shard_map/finish/pallas_call | solution.py:852

commit v7 on v6

--- a/solution.py
+++ b/solution.py
@@ -133,9 +133,9 @@
         self.here.add((dz, g))
 
     def load(self, dz, tile, sem):
-        for g in range(len(self.groups)):
+        for g, (lo, hi) in enumerate(self.groups):
             self.ready(dz, g)
-        self.bring(dz, 0, NR, tile, sem)
+            self.bring(dz, lo, hi - lo, tile.at[pl.ds(lo, hi - lo)], sem)
 
     def bring(self, dz, lo, n, tile, sem):
         for cc in range(NC):
@@ -265,8 +265,8 @@
     ta=((NR, NC, HB // 2, CUT), BF16), tb=((NR, NC, NR // 2, SUB, ROWS - CUT), BF16), s2a=((NR, HB, CUT), BF16), s2b=((NR, NR, SUB, ROWS - CUT), BF16),
     a2=((NR, NR - 1, SUB, CUT), BF16), b2=((NR, NR - 1, SUB, ROWS - CUT), BF16), fs=((NR, NC, FEATS, ROWS), BF16))
 ONE, EACH, BY_GROUP = (), (NR,), (NG,)
-SEMS = dict(f_s=ONE, fin_l=ONE, s_s=EACH, s_r=EACH, own_l=EACH, q_s=ONE, kw_s=ONE, kw_z=ONE, kw_y=ONE, kw_c=EACH, q_r=ONE, kv_s=ONE, kv_r=ONE, o_s=ONE, o_r=ONE, fin_s=ONE, out_l=ONE,
-            a1s=EACH, b1s=EACH, a2s=EACH, a2r=EACH, b2s=EACH, b2r=EACH, ag_s=BY_GROUP, ag_r=(NG, NG), tas=EACH, tbs=EACH, tar=(NR, NC), tbr=(NR, NC), b1r=(NR, NC), a1r=(NR, NC), ld=EACH, wsem=EACH, osem=EACH, vsem=BY_GROUP,
+SEMS = dict(f_s=ONE, fin_l=ONE, s_s=(NC,), s_r=(NC,), own_l=(NC,), q_s=ONE, kw_s=ONE, kw_z=ONE, kw_y=ONE, kw_c=(NC,), q_r=ONE, kv_s=ONE, kv_r=ONE, o_s=ONE, o_r=ONE, fin_s=ONE, out_l=ONE,
+            a1s=EACH, b1s=EACH, a2s=EACH, a2r=EACH, b2s=EACH, b2r=EACH, ag_s=BY_GROUP, ag_r=(NG, 6), tas=EACH, tbs=EACH, tar=(NR, NC), tbr=(NR, NC), b1r=(NR, NC), a1r=(NR, NC), ld=EACH, wsem=EACH, osem=(NC,), vsem=BY_GROUP,
             f_r=(NC, NG), fin_r=BY_GROUP)
 
 
@@ -280,7 +280,7 @@
     pos = z, y, x, c = tuple(lax.axis_index(a) for a in 'zyxc')
     flow = lambda kind, land, src, *more: kind(land, src, [rest.pop(0) for _ in WIDE_SEMS], pos, *more)
     fq = flow(Narrow, b.Q, (wq,))
-    fg, fu, fd = flow(Wide, b.G, wg), flow(Wide, b.U, wu), flow(Wide, b.D, wdT, SINGLE)
+    fg, fu, fd = flow(Wide, b.G, wg), flow(Wide, b.U, wu, SINGLE), flow(Wide, b.D, wdT, SINGLE)
     fo = flow(Narrow, b.O, (woT,))
     me = y * 4 + x
     row_low = lax.broadcasted_iota(jnp.int32, (FEATS, LANE), 1) < HALF
@@ -483,6 +483,7 @@
     fu.forward(0)
     fetch(fg, 1, 0)
     project(b.gacc, 1, 0, 0, 3 * TILE)
+    fu.z_send(3)
     fu.z_send(2)
     stage(3)
     turn(3)
@@ -574,6 +575,7 @@
             for dz in planes:
                 fd.z_put(g, dz)
 
+    fu.forward(3)
     fu.forward(2)
     fo.z_second()
     fetch(fu, 1, 1)
@@ -583,6 +585,7 @@
     start_d((2, SIDES))
     fu.last(0)
     fu.last(1)
+    fu.last(3)
     fu.last(2)
     fetch(fu, 3, 1)
     load_o = lambda i: fo.load(ORDER[i], b.wo_t.at[i % 2], b.osem.at[i % 2])
@@ -845,7 +848,7 @@
             out_shape=[shape(a) for a in outs],
             in_specs=[hbm, vmem, smem] + [hbm] * 9,
             out_specs=[hbm] * len(outs),
-            scratch_shapes=[pltpu.VMEM(*a) for a in VMEM_BUFS.values()] + [DMA(s) if s else DMA for s in SEMS.values()] + NARROW_SEMS + WIDE_SEMS * 2 + SINGLE_SEMS + NARROW_SEMS,
+            scratch_shapes=[pltpu.VMEM(*a) for a in VMEM_BUFS.values()] + [DMA(s) if s else DMA for s in SEMS.values()] + NARROW_SEMS + WIDE_SEMS + SINGLE_SEMS * 2 + NARROW_SEMS,
             name='decode_layer',
             compiler_params=pltpu.CompilerParams(collective_id=0, has_side_effects=True, vmem_limit_bytes=67043328),
         )(residual.T, ln_scale.reshape(1, FEATS), lengths, w_query, w_key, w_value, w_gate, w_up, w_down.T, w_out.T, k_cache, v_cache)

time: 248 us -> 248 us (level)
  no operation moved by 1% of the time
where the time goes in v7:
time: 248 us
  Pallas kernels  247 us (100%)
    pallas_call x1, Pallas kernels, layer(): pl.pallas_call(kernel, out_shape=[shape(a) for a in outs], in_specs=[hbm,...  244 us

profile of v7, /device:TPU:1, one launch (start us, length us, event | category | flops | bytes accessed | tf_op | source)
XLA Modules:
  0.0 247.8 jit_solution(15230433418223227190)
XLA Ops:
  0.6 244.0 %decode_layer.1 = (bf16[8,40,1024]{2,1,0:T(8,128)(2,1)}, bf16[64,64,128]{2,1,0:T(8,128)(2,1)}, bf16[64,64,128]{2,1,0:T(8,128)(2,1)}, bf16[8,320,640]{2,1,0:T(8,1...) custom-call(bf16[40,8192]{1,0:T(8,128)(2,1)} %bitcast.6, ...), custom_call_target="tpu_custom_call" | custom-call | tf_op jit(solution)/shard_map/decode_layer/pallas_call | solution.py:846
  244.6 3.0 %finish.1 = (bf16[40,8192]{1,0:T(8,128)(2,1)}, bf16[64,64,128]{2,1,0:T(8,128)(2,1)}, bf16[64,64,128]{2,1,0:T(8,128)(2,1)}) custom-call(bf16[8,40,1024]{2,1,0:T(8,128)(2,1)} %get-tuple-element.9.fin, bf16[64,64,128]{2,1,0:T(8,128)(2,1)} %get-tuple-element.10.kc_h, bf16[64,64,128]{2,1,0:T(8,128)(2,1)} %get-tuple-element.11.vc_h), custom_call_target="tpu_custom_call" | custom-call | tf_op jit(solution)/shard_map/finish/pallas_call | solution.py:855
